TPU v7x, 32 devices: a whole 2x2x4 slice. The times are simulated.
32 devices in a mesh: gx: 4 (over y, x), gy: 2 (over core), gz: 4 (over z).
Axes of the slice: x: 2, y: 2, z: 4, core: 2. Of those that a mesh axis runs over, the one named last changes fastest.
Arguments:
- rhs: float32 [3, 32, 32, 512], P(None, 'gx', 'gy', 'gz'), may hold values from -24 to 24
- conductivity: float32 [8], replicated, may hold values from 0.1 to 10
- fraction: float32 [3, 32, 32, 512], P(None, 'gx', 'gy', 'gz'), may hold values from 0.5 to 2
- region: int32 [32, 32, 512], P('gx', 'gy', 'gz'), may hold values from 0 to 7
- flags: int32 [3, 32, 32, 512], P(None, 'gx', 'gy', 'gz'), may hold values 0 or 1
Outputs:
- preconditioned: float32 [3, 32, 32, 512], P(None, 'gx', 'gy', 'gz')
All inputs are finite; a program needn't handle non-finite values. No bound on the sum of `flags` on one device may be relied on, other than what follows from the above.
Results may differ from a plain program's by a relative error of at most 0.00002.
Values sent between devices are 32-bit elements; how exact they have to be, the bound alone decides.
A program may use at most 64 MiB of HBM per device.

v0:
```python
import functools

import jax
import jax.numpy as jnp
from jax import lax
from jax.experimental import pallas as pl
from jax.experimental.pallas import tpu as pltpu
from jax.sharding import PartitionSpec as P

damping = 0.8
c_node = 0.8 / 7.0
MESH = pl.DeviceIdType.MESH
PAD = 4
SEG = 16


def rot(v, shift, axis):
    return pltpu.roll(v, shift % v.shape[axis], axis)


def y_up(v):
    return rot(v, -1, 0)


def y_down(v):
    return rot(v, 1, 0)


def z_up(v):
    return rot(v, -1, 1)


def z_down(v):
    return rot(v, 1, 1)


def face_zero(u1, u2):
    return (y_up(u2) - u2) - (z_up(u1) - u1)


def face_one(u0, u2, u2p):
    return (z_up(u0) - u0) - (u2p - u2)


def face_two(u0, u1, u1p):
    return (u1p - u1) - (y_up(u0) - u0)


def edges(f0, f1, f2, f1m, f2m):
    return (
        (z_down(f1) - f1) - (y_down(f2) - f2),
        (f2m - f2) - (z_down(f0) - f0),
        (y_down(f0) - f0) - (f1m - f1),
    )


def jacobi_scale(ks):
    return damping / jnp.where(ks > 0.0, 4.0 + ks, 1.0)


def start_iter(rhs, ks):
    return jnp.where(ks > 0.0, jacobi_scale(ks) * rhs, 0.0)


def next_iter(rhs, ks, u, cc):
    new = u + jacobi_scale(ks) * (rhs - (cc + ks * u))
    return jnp.where(ks > 0.0, new, 0.0)


def masked_residual(rhs, ks, u, cc):
    return jnp.where(ks > 0.0, rhs - (cc + ks * u), 0.0)


def nodal_rhs(m0, m0m, m1, m2):
    m1m, m2m = y_down(m1), z_down(m2)
    return (
        (m0m - m0) + (m1m - m1) + (m2m - m2),
        (m0 + m0m) * 0.5,
        (m1 + m1m) * 0.5,
        (m2 + m2m) * 0.5,
    )


def nodal_step(r, rm, rp):
    around = (rm + rp) + (y_up(r) + y_down(r)) + (z_up(r) + z_down(r))
    return (1.2 * c_node) * r + (c_node * c_node) * around


def finish(rhs, ks, u, corr):
    fixed = damping * rhs
    fixed = fixed + damping * (rhs - fixed)
    return jnp.where(ks > 0.0, u + corr, fixed)


def kernel(
    sizes, nx, ny, nz, cond, rhs_hbm, frac_hbm, reg_hbm, flag_hbm, out_ref,
    rhs_ref, frac_ref, reg_ref, flag_ref,
    e, w, wz, kf, ds, dr, ya, yb, yra, yrb, u1, u2, mm, rr, load, send, recv,
):
    gx, gy, gz = sizes
    pos = {"gx": lax.axis_index("gx"), "gy": lax.axis_index("gy"), "gz": lax.axis_index("gz")}
    size = {"gx": gx, "gy": gy, "gz": gz}
    tiles = nx * SEG // nz
    planes = nx + 2 * PAD
    per = nz // SEG

    def device(**steps):
        return {axis: lax.rem(pos[axis] + (step + size[axis]), size[axis]) for axis, step in steps.items()}

    partners = [device(gx=1), device(gx=-1), device(gz=1), device(gz=-1), device(gy=1)]
    if gy > 2:
        partners.append(device(gy=-1))
    barrier = pltpu.get_barrier_semaphore()
    for partner in partners:
        pl.semaphore_signal(barrier, inc=1, device_id=partner, device_id_type=MESH)
    loads = [
        pltpu.make_async_copy(src, dst, load.at[i])
        for i, (src, dst) in enumerate(
            ((reg_hbm, reg_ref), (frac_hbm, frac_ref), (flag_hbm, flag_ref), (rhs_hbm, rhs_ref))
        )
    ]
    for one in loads:
        one.start()
    for one in loads:
        one.wait()

    lane = lax.broadcasted_iota(jnp.int32, (ny, nz), 1)
    slot = lane // SEG
    half = nz // 2
    low_half = lane < half
    quad = (lane % SEG) // 4
    left = (lane % SEG) < 8

    def end_piece(v, j):
        return rot(v, 8 + SEG * j, 1)

    packs = [[None] * tiles for _ in range(6)]
    outer = {nx - 3: 0, 3: 1}
    for x in range(nx):
        region = reg_ref[x]
        sigma = jnp.zeros((ny, nz), jnp.float32)
        for number in range(cond.shape[0]):
            sigma = jnp.where(region == number, cond[number], sigma)
        t, j = divmod(x, per)
        for k in range(3):
            ks = jnp.where(flag_ref[k, x] == 0, sigma * frac_ref[k, x], 0.0)
            rhs = rhs_ref[k, x]
            for f, v in ((k, rhs), (3 + k, ks)):
                e[f, PAD + x, 0:ny, :] = v
                piece = end_piece(v, j)
                old = packs[f][t]
                packs[f][t] = piece if old is None else jnp.where(slot == j, piece, old)
            if x in outer:
                kf[outer[x], k] = start_iter(rhs, ks)
    for f in range(6):
        for t in range(tiles):
            w[f, t] = packs[f][t]
    pl.semaphore_wait(barrier, len(partners))

    def copy(number, src, dst, where):
        made = pltpu.make_async_remote_copy(
            src_ref=src, dst_ref=dst, send_sem=send.at[number], recv_sem=recv.at[number],
            device_id=where, device_id_type=MESH,
        )
        made.start()
        return made

    own_rows = pl.ds(0, ny)
    z_copies = [copy(0, w, wz.at[0], device(gz=1)), copy(1, w, wz.at[1], device(gz=-1))]
    x_copies = [
        copy(6, e.at[:, pl.ds(PAD + nx - 2, 2), own_rows], e.at[:, pl.ds(2, 2), own_rows], device(gx=1)),
        copy(7, e.at[:, pl.ds(PAD, 3), own_rows], e.at[:, pl.ds(PAD + nx, 3), own_rows], device(gx=-1)),
        copy(8, kf.at[0], e.at[pl.ds(0, 3), 1, own_rows], device(gx=1)),
        copy(9, kf.at[1, pl.ds(1, 2)], e.at[pl.ds(1, 2), PAD + nx + 3, own_rows], device(gx=-1)),
    ]

    base_a = planes
    base_b = planes + tiles + 1
    row = lax.broadcasted_iota(jnp.int32, (8, nz), 0)

    def y_start(first, which, out, into):
        for f in range(6):
            for i, p in enumerate(which):
                out[f, i] = jnp.where(row < 4, e[f, p, 0:8, :], e[f, p, ny - 8:ny, :])
        if gy == 2:
            return [copy(first, out, into.at[0], device(gy=1))]
        return [
            copy(first, out, into.at[0], device(gy=-1)),
            copy(first + 1, out, into.at[1], device(gy=1)),
        ]

    def y_finish(copies, which, into):
        for one in copies:
            one.wait()
        for f in range(6):
            for i, p in enumerate(which):
                tile = into[0, f, i] if gy == 2 else jnp.where(row < 4, into[0, f, i], into[1, f, i])
                e[f, p, ny:ny + 8, :] = tile

    def curl_sweep(u, lo, hi, emit):
        def faces(p):
            v0, v1, v2 = u[0, p], u[1, p], u[2, p]
            return face_one(v0, v2, u[2, p + 1]), face_two(v0, v1, u[1, p + 1])

        f1m, f2m = faces(lo - 1)
        for p in range(lo, hi):
            f1, f2 = faces(p)
            f0 = face_zero(u[1, p], u[2, p])
            cc = edges(f0, f1, f2, f1m, f2m)
            for k in range(3):
                emit(k, p, cc[k])
            f1m, f2m = f1, f2

    def emit_second(k, p, cc):
        u2[k, p] = next_iter(e[k, p], e[3 + k, p], u1[k, p], cc)

    def emit_masked(k, p, cc):
        mm[k, p] = masked_residual(e[k, p], e[3 + k, p], u2[k, p], cc)

    def node_range(lo, hi):
        for p in range(lo, hi):
            r = nodal_rhs(mm[0, p], mm[0, p - 1], mm[1, p], mm[2, p])
            for q in range(4):
                rr[q, p] = r[q]

    def first_range(which):
        for p in which:
            for k in range(3):
                u1[k, p] = start_iter(e[k, p], e[3 + k, p])

    own = list(range(PAD, PAD + nx))
    y_own = y_start(10, own, ya, yra)
    y_finish(y_own, own, yra)
    first_range(own)
    for one in z_copies:
        one.wait()
    for side in range(2):
        mine = (lane >= half) if side == 0 else low_half
        j = (nx - 3) % per if side == 0 else 3
        t = tiles - 1 if side == 0 else 0
        for zside, off in ((0, 8), (1, 4)):
            tile = None
            for f in range(6):
                v = wz[1 - zside, f, t]
                if f < 3:
                    v = jnp.where(slot == j, start_iter(v, wz[1 - zside, 3 + f, t]), v)
                moved = rot(v, 4 * (f % 4) - off + (half if f >= 4 else 0), 1)
                where = (quad == f % 4) & (mine if f < 4 else ~mine)
                tile = moved if tile is None else jnp.where(where, moved, tile)
            ds[side, zside] = tile
    x_copies += [copy(2 + side, ds.at[side], dr.at[side], device(gx=1 - 2 * side)) for side in range(2)]
    for f in range(6):
        for t in range(tiles):
            mid = w[f, t]
            e[f, base_a + t, 0:ny, :] = jnp.where(left, mid, wz[1, f, t])
            e[f, base_b + t, 0:ny, :] = jnp.where(left, wz[0, f, t], mid)
    curl_sweep(u1, PAD + 1, PAD + nx - 1, emit_second)
    curl_sweep(u2, PAD + 2, PAD + nx - 2, emit_masked)
    node_range(PAD + 3, PAD + nx - 2)

    for one in x_copies:
        one.wait()
    for f in range(6):
        ends = None
        for i in range(8):
            if i != 4:
                p = PAD + nx + i if i < 4 else i - 4
                piece = end_piece(e[f, p, 0:ny, :], i)
                ends = piece if ends is None else jnp.where(slot == i, piece, ends)
        corner = []
        for zside, off in ((0, 8), (1, 4)):
            plus, minus = dr[1, zside], dr[0, zside]
            if f < 4:
                corner.append(rot(jnp.where(low_half, plus, minus), off - 4 * f, 1))
            else:
                corner.append(rot(jnp.where(low_half, minus, plus), half + off - 4 * (f - 4), 1))
        e[f, base_a + tiles, 0:ny, :] = jnp.where(left, ends, corner[0])
        e[f, base_b + tiles, 0:ny, :] = jnp.where(left, corner[1], ends)
    rest = list(range(1, PAD)) + list(range(PAD + nx, planes)) + list(range(base_a, base_b + tiles + 1))
    y_rest = y_start(12, rest, yb, yrb)
    y_finish(y_rest, rest, yrb)

    lane24 = lax.broadcasted_iota(jnp.int32, (ny + 8, nz), 1)

    sent = (lane24 // SEG == 3) | (lane24 // SEG == 5)

    def x_up(vs):
        rs = [rot(v, -SEG, 1) for v in vs]
        return [jnp.where(lane24 < nz - SEG, rs[t], rs[(t + 1) % len(rs)]) for t in range(len(rs))]

    def x_down(vs):
        rs = [rot(v, SEG, 1) for v in vs]
        return [jnp.where(lane24 >= SEG, rs[t], rs[t - 1]) for t in range(len(rs))]

    count = tiles + 1

    def strip_curl(u):
        u1p, u2p = x_up(u[1]), x_up(u[2])
        f0 = [face_zero(u[1][t], u[2][t]) for t in range(count)]
        f1 = [face_one(u[0][t], u[2][t], u2p[t]) for t in range(count)]
        f2 = [face_two(u[0][t], u[1][t], u1p[t]) for t in range(count)]
        f1m, f2m = x_down(f1), x_down(f2)
        out = [edges(f0[t], f1[t], f2[t], f1m[t], f2m[t]) for t in range(count)]
        return [[out[t][k] for t in range(count)] for k in range(3)]

    ends = []
    for base in (base_a, base_b):
        def sr(k, t):
            return e[k, base + t]

        def sk(k, t):
            return e[3 + k, base + t]

        span = range(count)
        u = [[start_iter(sr(k, t), sk(k, t)) for t in span] for k in range(3)]
        for k in range(3):
            u[k][tiles] = jnp.where(sent, sr(k, tiles), u[k][tiles])
        cc = strip_curl(u)
        u = [[next_iter(sr(k, t), sk(k, t), u[k][t], cc[k][t]) for t in span] for k in range(3)]
        cc = strip_curl(u)
        m = [[masked_residual(sr(k, t), sk(k, t), u[k][t], cc[k][t]) for t in span] for k in range(3)]
        m0m = x_down(m[0])
        r = [nodal_rhs(m[0][t], m0m[t], m[1][t], m[2][t]) for t in span]
        s = []
        for q in range(4):
            rq = [r[t][q] for t in span]
            rm, rp = x_down(rq), x_up(rq)
            s.append([nodal_step(rq[t], rm[t], rp[t]) for t in span])
        s0p, s1p = x_up(s[0]), x_up(s[1])
        result = []
        for t in range(tiles):
            corr = (
                (s0p[t] - s[0][t]) + (s[1][t] + s1p[t]) * 0.5,
                (y_up(s[0][t]) - s[0][t]) + (s[2][t] + y_up(s[2][t])) * 0.5,
                (z_up(s[0][t]) - s[0][t]) + (s[3][t] + z_up(s[3][t])) * 0.5,
            )
            result.append([finish(sr(k, t), sk(k, t), u[k][t], corr[k])[0:ny] for k in range(3)])
        ends.append(result)
    for t in range(tiles):
        for k in range(3):
            w[k, t] = jnp.where(left, ends[0][t][k], ends[1][t][k])

    for k in range(3):
        u1[k, 1] = e[k, 1]
        u1[k, planes - 1] = e[k, planes - 1]
    first_range(list(range(2, PAD)) + list(range(PAD + nx, planes - 1)))
    curl_sweep(u1, PAD - 2, PAD + 1, emit_second)
    curl_sweep(u1, PAD + nx - 1, PAD + nx + 3, emit_second)
    curl_sweep(u2, PAD - 1, PAD + 2, emit_masked)
    curl_sweep(u2, PAD + nx - 2, PAD + nx + 2, emit_masked)
    p = PAD - 2
    v0, v1, v2 = u2[0, p], u2[1, p], u2[2, p]
    f1 = face_one(v0, v2, u2[2, p + 1])
    f2 = face_two(v0, v1, u2[1, p + 1])
    emit_masked(0, p, (z_down(f1) - f1) - (y_down(f2) - f2))
    node_range(PAD - 1, PAD + 3)
    node_range(PAD + nx - 2, PAD + nx + 2)

    inner = (lane >= 4) & (lane < nz - 4)
    s_next = [nodal_step(rr[q, PAD], rr[q, PAD - 1], rr[q, PAD + 1]) for q in range(4)]
    for x in range(nx):
        p = PAD + x
        s = s_next
        s_next = [nodal_step(rr[q, p + 1], rr[q, p], rr[q, p + 2]) for q in range(4)] if x < nx - 1 else [
            nodal_step(rr[q, p + 1], rr[q, p], rr[q, p + 2]) for q in range(2)
        ]
        corr = (
            (s_next[0] - s[0]) + (s[1] + s_next[1]) * 0.5,
            (y_up(s[0]) - s[0]) + (s[2] + y_up(s[2])) * 0.5,
            (z_up(s[0]) - s[0]) + (s[3] + z_up(s[3])) * 0.5,
        )
        t, j = divmod(x, per)
        for k in range(3):
            body = finish(e[k, p, 0:ny], e[3 + k, p, 0:ny], u2[k, p, 0:ny], corr[k][0:ny])
            out_ref[k, x] = jnp.where(inner, body, rot(w[k, t], nz - 8 - SEG * j, 1))


def on_device(sizes, rhs, conductivity, fraction, region, flags):
    _, nx, ny, nz = rhs.shape
    tiles = nx * SEG // nz
    planes = nx + 2 * PAD
    total = planes + 2 * (tiles + 1)
    rest = 2 * PAD - 1 + 2 * (tiles + 1)
    rows = ny + 8
    f32 = jnp.float32
    hbm = pl.BlockSpec(memory_space=pl.ANY)
    sides = 1 if sizes[1] == 2 else 2
    return pl.pallas_call(
        functools.partial(kernel, sizes, nx, ny, nz),
        out_shape=pltpu.VMEM(rhs.shape, rhs.dtype),
        in_specs=[pl.BlockSpec(memory_space=pltpu.SMEM)] + [hbm] * 4,
        out_specs=pl.BlockSpec(memory_space=pltpu.VMEM),
        scratch_shapes=[
            pltpu.VMEM(rhs.shape, f32),
            pltpu.VMEM(rhs.shape, f32),
            pltpu.VMEM(region.shape, jnp.int32),
            pltpu.VMEM(flags.shape, jnp.int32),
            pltpu.VMEM((6, total, rows, nz), f32),
            pltpu.VMEM((6, tiles, ny, nz), f32),
            pltpu.VMEM((2, 6, tiles, ny, nz), f32),
            pltpu.VMEM((2, 3, ny, nz), f32),
            pltpu.VMEM((2, 2, ny, nz), f32),
            pltpu.VMEM((2, 2, ny, nz), f32),
            pltpu.VMEM((6, nx, 8, nz), f32),
            pltpu.VMEM((6, rest, 8, nz), f32),
            pltpu.VMEM((sides, 6, nx, 8, nz), f32),
            pltpu.VMEM((sides, 6, rest, 8, nz), f32),
            pltpu.VMEM((3, planes, rows, nz), f32),
            pltpu.VMEM((3, planes, rows, nz), f32),
            pltpu.VMEM((3, planes, rows, nz), f32),
            pltpu.VMEM((4, planes, rows, nz), f32),
            pltpu.SemaphoreType.DMA((4,)),
            pltpu.SemaphoreType.DMA((14,)),
            pltpu.SemaphoreType.DMA((14,)),
        ],
        compiler_params=pltpu.CompilerParams(
            collective_id=0, has_side_effects=True, vmem_limit_bytes=60 * 1024 * 1024
        ),
    )(conductivity, rhs, fraction, region, flags)


def solution(mesh):
    sizes = tuple(mesh.shape[name] for name in ("gx", "gy", "gz"))
    return jax.shard_map(
        functools.partial(on_device, sizes),
        mesh=mesh,
        in_specs=(
            P(None, "gx", "gy", "gz"),
            P(),
            P(None, "gx", "gy", "gz"),
            P("gx", "gy", "gz"),
            P(None, "gx", "gy", "gz"),
        ),
        out_specs=P(None, "gx", "gy", "gz"),
        check_vma=False,
    )
```

profile of v0, /device:TPU:0, one launch (start us, length us, event | category | flops | bytes accessed | tf_op | source)
XLA Modules:
  0.0 19.9 jit_solution(1218249245601605247)
XLA Ops:
  0.0 19.2 %shard_map.55 = f32[3,8,16,128]{3,2,1,0:T(8,128)S(1)} custom-call(f32[8]{0:T(128)} %cond.1, f32[3,8,16,128]{3,2,1,0:T(8,128)} %rhs_hbm.1, f32[3,8,16,128]{3,2,1,0:T(8,128)} %frac_hbm.1, s32[8,16,128]{2,1,0:T(8,128)} %reg_hbm.1, s32[3,8,16,128]{3,2,1,0:T(8,128)} %flag_hbm.1), custom_call_target="tpu_custom_call" | custom-call | tf_op jit(solution)/shard_map/pallas_call | solution.py:388
  19.2 0.7 %copy.7 = f32[3,8,16,128]{3,2,1,0:T(8,128)} copy(f32[3,8,16,128]{3,2,1,0:T(8,128)S(1)} %shard_map.55) | data formatting | bytes 393216
where the time goes:
time: 20.1 us; the launch traced here: 19.9 us
  Pallas kernels  19.2 us (96%)
  local copies, waits for them, and re-layouts  0.68 us (3%)
    pallas_call x1, Pallas kernels, on_device(): pl.pallas_call(functools.partial(kernel, sizes, nx, ny, nz), out_shape=pl...  19.2 us
    unnamed x1, local copies, waits for them, and re-layouts  0.68 us

commit v1 on v0

--- a/solution.py
+++ b/solution.py
@@ -93,9 +93,9 @@
 
 
 def kernel(
-    sizes, nx, ny, nz, cond, rhs_hbm, frac_hbm, reg_hbm, flag_hbm, out_ref,
-    rhs_ref, frac_ref, reg_ref, flag_ref,
-    e, w, wz, kf, ds, dr, ya, yb, yra, yrb, u1, u2, mm, rr, load, send, recv,
+    sizes, nx, ny, nz, cond_hbm, rhs_hbm, frac_hbm, reg_hbm, flag_hbm, out_ref,
+    cond, rhs_ref, frac_ref, reg_ref, flag_ref,
+    e, w, wz, kf, ds, dr, ya, yb, yra, yrb, u1, u2, mm, rr, load, send, recv, near,
 ):
     gx, gy, gz = sizes
     pos = {"gx": lax.axis_index("gx"), "gy": lax.axis_index("gy"), "gz": lax.axis_index("gz")}
@@ -107,22 +107,35 @@
     def device(**steps):
         return {axis: lax.rem(pos[axis] + (step + size[axis]), size[axis]) for axis, step in steps.items()}
 
-    partners = [device(gx=1), device(gx=-1), device(gz=1), device(gz=-1), device(gy=1)]
+    partners = [device(gx=1), device(gx=-1), device(gy=1)]
     if gy > 2:
         partners.append(device(gy=-1))
+    steps = [(x, z) for z in (1, -1) for x in (0, 1, -1)]
+    far = [device(gx=x, gz=z) for x, z in steps]
+    alternate = gz % 2 == 0
+    early = lax.rem(pos["gz"], 2) == 0
     barrier = pltpu.get_barrier_semaphore()
-    for partner in partners:
-        pl.semaphore_signal(barrier, inc=1, device_id=partner, device_id_type=MESH)
+
+    def greet(devices):
+        for one in devices:
+            pl.semaphore_signal(barrier, inc=1, device_id=one, device_id_type=MESH)
+
+    greet(partners)
+    if alternate:
+        pl.when(early)(lambda: greet(far))
+    else:
+        greet(far)
     loads = [
         pltpu.make_async_copy(src, dst, load.at[i])
         for i, (src, dst) in enumerate(
-            ((reg_hbm, reg_ref), (frac_hbm, frac_ref), (flag_hbm, flag_ref), (rhs_hbm, rhs_ref))
+            ((cond_hbm, cond), (reg_hbm, reg_ref), (frac_hbm, frac_ref), (flag_hbm, flag_ref), (rhs_hbm, rhs_ref))
         )
     ]
-    for one in loads:
-        one.start()
-    for one in loads:
-        one.wait()
+    with jax.named_scope("load"):
+        for one in loads:
+            one.start()
+        for one in loads:
+            one.wait()
 
     lane = lax.broadcasted_iota(jnp.int32, (ny, nz), 1)
     slot = lane // SEG
@@ -155,7 +168,31 @@
     for f in range(6):
         for t in range(tiles):
             w[f, t] = packs[f][t]
-    pl.semaphore_wait(barrier, len(partners))
+    for side in range(2):
+        mine = (lane >= half) if side == 0 else low_half
+        j = (nx - 3) % per if side == 0 else 3
+        t = tiles - 1 if side == 0 else 0
+        for zside, off in ((0, 8), (1, 4)):
+            tile = None
+            for f in range(6):
+                v = packs[f][t]
+                if f < 3:
+                    v = jnp.where(slot == j, start_iter(v, packs[3 + f][t]), v)
+                moved = rot(v, 4 * (f % 4) - off + (half if f >= 4 else 0), 1)
+                where = (quad == f % 4) & (mine if f < 4 else ~mine)
+                tile = moved if tile is None else jnp.where(where, moved, tile)
+            ds[side, zside] = tile
+    with jax.named_scope("barrierwait"):
+        if alternate:
+            pl.semaphore_wait(barrier, jnp.where(early, len(partners), len(partners) + len(far)))
+
+            @pl.when(jnp.logical_not(early))
+            def _():
+                for i, (x, z) in enumerate(steps):
+                    there = steps.index((-x, -z))
+                    pl.semaphore_signal(near.at[there], inc=1, device_id=far[i], device_id_type=MESH)
+        else:
+            pl.semaphore_wait(barrier, len(partners) + len(far))
 
     def copy(number, src, dst, where):
         made = pltpu.make_async_remote_copy(
@@ -166,12 +203,11 @@
         return made
 
     own_rows = pl.ds(0, ny)
-    z_copies = [copy(0, w, wz.at[0], device(gz=1)), copy(1, w, wz.at[1], device(gz=-1))]
     x_copies = [
         copy(6, e.at[:, pl.ds(PAD + nx - 2, 2), own_rows], e.at[:, pl.ds(2, 2), own_rows], device(gx=1)),
         copy(7, e.at[:, pl.ds(PAD, 3), own_rows], e.at[:, pl.ds(PAD + nx, 3), own_rows], device(gx=-1)),
-        copy(8, kf.at[0], e.at[pl.ds(0, 3), 1, own_rows], device(gx=1)),
-        copy(9, kf.at[1, pl.ds(1, 2)], e.at[pl.ds(1, 2), PAD + nx + 3, own_rows], device(gx=-1)),
+        copy(14, kf.at[0], e.at[pl.ds(0, 3), 1, own_rows], device(gx=1)),
+        copy(15, kf.at[1, pl.ds(1, 2)], e.at[pl.ds(1, 2), PAD + nx + 3, own_rows], device(gx=-1)),
     ]
 
     base_a = planes
@@ -229,37 +265,39 @@
                 u1[k, p] = start_iter(e[k, p], e[3 + k, p])
 
     own = list(range(PAD, PAD + nx))
-    y_own = y_start(10, own, ya, yra)
-    y_finish(y_own, own, yra)
-    first_range(own)
-    for one in z_copies:
-        one.wait()
-    for side in range(2):
-        mine = (lane >= half) if side == 0 else low_half
-        j = (nx - 3) % per if side == 0 else 3
-        t = tiles - 1 if side == 0 else 0
-        for zside, off in ((0, 8), (1, 4)):
-            tile = None
-            for f in range(6):
-                v = wz[1 - zside, f, t]
-                if f < 3:
-                    v = jnp.where(slot == j, start_iter(v, wz[1 - zside, 3 + f, t]), v)
-                moved = rot(v, 4 * (f % 4) - off + (half if f >= 4 else 0), 1)
-                where = (quad == f % 4) & (mine if f < 4 else ~mine)
-                tile = moved if tile is None else jnp.where(where, moved, tile)
-            ds[side, zside] = tile
-    x_copies += [copy(2 + side, ds.at[side], dr.at[side], device(gx=1 - 2 * side)) for side in range(2)]
+    with jax.named_scope("y1"):
+        y_own = y_start(10, own, ya, yra)
+        y_finish(y_own, own, yra)
+    with jax.named_scope("inner"):
+        first_range(own)
+        curl_sweep(u1, PAD + 1, PAD + nx - 1, emit_second)
+        curl_sweep(u2, PAD + 2, PAD + nx - 2, emit_masked)
+        node_range(PAD + 3, PAD + nx - 2)
+    with jax.named_scope("nearwait"):
+        if alternate:
+            @pl.when(early)
+            def _():
+                for i in range(len(steps)):
+                    pl.semaphore_wait(near.at[i], 1)
+    z_copies = [copy(0, w, wz.at[0], device(gz=1)), copy(1, w, wz.at[1], device(gz=-1))]
+    corner_copies = [
+        copy(2 + 2 * side + zside, ds.at[side, zside], dr.at[side, zside], device(gx=1 - 2 * side, gz=2 * zside - 1))
+        for side in range(2) for zside in range(2)
+    ]
+    with jax.named_scope("zwait"):
+        for one in z_copies:
+            one.wait()
     for f in range(6):
         for t in range(tiles):
             mid = w[f, t]
             e[f, base_a + t, 0:ny, :] = jnp.where(left, mid, wz[1, f, t])
             e[f, base_b + t, 0:ny, :] = jnp.where(left, wz[0, f, t], mid)
-    curl_sweep(u1, PAD + 1, PAD + nx - 1, emit_second)
-    curl_sweep(u2, PAD + 2, PAD + nx - 2, emit_masked)
-    node_range(PAD + 3, PAD + nx - 2)
-
-    for one in x_copies:
-        one.wait()
+    with jax.named_scope("xwait"):
+        for one in x_copies:
+            one.wait()
+    with jax.named_scope("cornerwait"):
+        for one in corner_copies:
+            one.wait()
     for f in range(6):
         ends = None
         for i in range(8):
@@ -277,8 +315,9 @@
         e[f, base_a + tiles, 0:ny, :] = jnp.where(left, ends, corner[0])
         e[f, base_b + tiles, 0:ny, :] = jnp.where(left, corner[1], ends)
     rest = list(range(1, PAD)) + list(range(PAD + nx, planes)) + list(range(base_a, base_b + tiles + 1))
-    y_rest = y_start(12, rest, yb, yrb)
-    y_finish(y_rest, rest, yrb)
+    with jax.named_scope("yrest"):
+        y_rest = y_start(12, rest, yb, yrb)
+        y_finish(y_rest, rest, yrb)
 
     lane24 = lax.broadcasted_iota(jnp.int32, (ny + 8, nz), 1)
 
@@ -303,6 +342,8 @@
         out = [edges(f0[t], f1[t], f2[t], f1m[t], f2m[t]) for t in range(count)]
         return [[out[t][k] for t in range(count)] for k in range(3)]
 
+    strips = jax.named_scope('strips')
+    strips.__enter__()
     ends = []
     for base in (base_a, base_b):
         def sr(k, t):
@@ -340,6 +381,9 @@
         for k in range(3):
             w[k, t] = jnp.where(left, ends[0][t][k], ends[1][t][k])
 
+    strips.__exit__(None, None, None)
+    outer_x = jax.named_scope('outerx')
+    outer_x.__enter__()
     for k in range(3):
         u1[k, 1] = e[k, 1]
         u1[k, planes - 1] = e[k, planes - 1]
@@ -356,6 +400,7 @@
     node_range(PAD - 1, PAD + 3)
     node_range(PAD + nx - 2, PAD + nx + 2)
 
+    outer_x.__exit__(None, None, None)
     inner = (lane >= 4) & (lane < nz - 4)
     s_next = [nodal_step(rr[q, PAD], rr[q, PAD - 1], rr[q, PAD + 1]) for q in range(4)]
     for x in range(nx):
@@ -388,9 +433,10 @@
     return pl.pallas_call(
         functools.partial(kernel, sizes, nx, ny, nz),
         out_shape=pltpu.VMEM(rhs.shape, rhs.dtype),
-        in_specs=[pl.BlockSpec(memory_space=pltpu.SMEM)] + [hbm] * 4,
+        in_specs=[hbm] * 5,
         out_specs=pl.BlockSpec(memory_space=pltpu.VMEM),
         scratch_shapes=[
+            pltpu.SMEM(conductivity.shape, f32),
             pltpu.VMEM(rhs.shape, f32),
             pltpu.VMEM(rhs.shape, f32),
             pltpu.VMEM(region.shape, jnp.int32),
@@ -409,9 +455,10 @@
             pltpu.VMEM((3, planes, rows, nz), f32),
             pltpu.VMEM((3, planes, rows, nz), f32),
             pltpu.VMEM((4, planes, rows, nz), f32),
-            pltpu.SemaphoreType.DMA((4,)),
-            pltpu.SemaphoreType.DMA((14,)),
-            pltpu.SemaphoreType.DMA((14,)),
+            pltpu.SemaphoreType.DMA((5,)),
+            pltpu.SemaphoreType.DMA((16,)),
+            pltpu.SemaphoreType.DMA((16,)),
+            pltpu.SemaphoreType.REGULAR((6,)),
         ],
         compiler_params=pltpu.CompilerParams(
             collective_id=0, has_side_effects=True, vmem_limit_bytes=60 * 1024 * 1024

time: 20.1 us -> 18.7 us (0.930)
  Pallas kernels: 19.2 us -> 17.9 us
    pallas_call x1, Pallas kernels: 19.2 us -> 17.9 us  [on_device(): pl.pallas_call(functools.partial(kernel, sizes, nx, ny, nz), out_shape=pl...]
where the time goes in v1:
time: 18.7 us; the launch traced here: 18.5 us
  Pallas kernels  17.9 us (96%)
  local copies, waits for them, and re-layouts  0.68 us (4%)
    pallas_call x1, Pallas kernels, on_device(): pl.pallas_call(functools.partial(kernel, sizes, nx, ny, nz), out_shape=pl...  17.9 us
    unnamed x1, local copies, waits for them, and re-layouts  0.68 us

profile of v1, /device:TPU:0, one launch (start us, length us, event | category | flops | bytes accessed | tf_op | source)
XLA Modules:
  0.0 18.5 jit_solution(8377920500214862179)
XLA Ops:
  0.0 17.9 %shard_map.55 = f32[3,8,16,128]{3,2,1,0:T(8,128)S(1)} custom-call(f32[8]{0:T(128)} %cond_hbm.1, f32[3,8,16,128]{3,2,1,0:T(8,128)} %rhs_hbm.1, f32[3,8,16,128]{3,2,1,0:T(8,128)} %frac_hbm.1, s32[8,16,128]{2,1,0:T(8,128)} %reg_hbm.1, s32[3,8,16,128]{3,2,1,0:T(8,128)} %flag_hbm.1), custom_call_target="tpu_custom_call" | custom-call | tf_op jit(solution)/shard_map/pallas_call | solution.py:433
  17.9 0.7 %copy.7 = f32[3,8,16,128]{3,2,1,0:T(8,128)} copy(f32[3,8,16,128]{3,2,1,0:T(8,128)S(1)} %shard_map.55) | data formatting | bytes 393216

commit v2 on v1

--- a/solution.py
+++ b/solution.py
@@ -194,21 +194,50 @@
         else:
             pl.semaphore_wait(barrier, len(partners) + len(far))
 
-    def copy(number, src, dst, where):
+    def copy(number, src, dst, where, start=True):
         made = pltpu.make_async_remote_copy(
             src_ref=src, dst_ref=dst, send_sem=send.at[number], recv_sem=recv.at[number],
             device_id=where, device_id_type=MESH,
         )
-        made.start()
+        if start:
+            made.start()
         return made
 
     own_rows = pl.ds(0, ny)
-    x_copies = [
-        copy(6, e.at[:, pl.ds(PAD + nx - 2, 2), own_rows], e.at[:, pl.ds(2, 2), own_rows], device(gx=1)),
-        copy(7, e.at[:, pl.ds(PAD, 3), own_rows], e.at[:, pl.ds(PAD + nx, 3), own_rows], device(gx=-1)),
-        copy(14, kf.at[0], e.at[pl.ds(0, 3), 1, own_rows], device(gx=1)),
-        copy(15, kf.at[1, pl.ds(1, 2)], e.at[pl.ds(1, 2), PAD + nx + 3, own_rows], device(gx=-1)),
+    up_copies = [
+        copy(6, e.at[:, pl.ds(PAD + nx - 2, 2), own_rows], e.at[:, pl.ds(2, 2), own_rows], device(gx=1), False),
+        copy(14, kf.at[0], e.at[pl.ds(0, 3), 1, own_rows], device(gx=1), False),
     ]
+    down_copies = [
+        copy(7, e.at[:, pl.ds(PAD, 3), own_rows], e.at[:, pl.ds(PAD + nx, 3), own_rows], device(gx=-1), False),
+        copy(15, kf.at[1, pl.ds(1, 2)], e.at[pl.ds(1, 2), PAD + nx + 3, own_rows], device(gx=-1), False),
+    ]
+    x_copies = up_copies + down_copies
+    up_first = lax.rem(pos["gx"], 4) == 3
+    z_copies = [copy(0, w, wz.at[0], device(gz=1), False), copy(1, w, wz.at[1], device(gz=-1), False)]
+    corner_copies = [
+        copy(2 + 2 * side + zside, ds.at[side, zside], dr.at[side, zside], device(gx=1 - 2 * side, gz=2 * zside - 1), False)
+        for side in range(2) for zside in range(2)
+    ]
+
+    def start_far():
+        for one in corner_copies + z_copies:
+            one.start()
+
+    if alternate:
+        pl.when(jnp.logical_not(early))(start_far)
+    else:
+        start_far()
+
+    @pl.when(up_first)
+    def _():
+        for one in up_copies + down_copies:
+            one.start()
+
+    @pl.when(jnp.logical_not(up_first))
+    def _():
+        for one in down_copies + up_copies:
+            one.start()
 
     base_a = planes
     base_b = planes + tiles + 1
@@ -279,14 +308,11 @@
             def _():
                 for i in range(len(steps)):
                     pl.semaphore_wait(near.at[i], 1)
-    z_copies = [copy(0, w, wz.at[0], device(gz=1)), copy(1, w, wz.at[1], device(gz=-1))]
-    corner_copies = [
-        copy(2 + 2 * side + zside, ds.at[side, zside], dr.at[side, zside], device(gx=1 - 2 * side, gz=2 * zside - 1))
-        for side in range(2) for zside in range(2)
-    ]
+                for one in z_copies + corner_copies:
+                    one.start()
     with jax.named_scope("zwait"):
         for one in z_copies:
-            one.wait()
+            one.wait_recv()
     for f in range(6):
         for t in range(tiles):
             mid = w[f, t]
@@ -294,10 +320,10 @@
             e[f, base_b + t, 0:ny, :] = jnp.where(left, wz[0, f, t], mid)
     with jax.named_scope("xwait"):
         for one in x_copies:
-            one.wait()
+            one.wait_recv()
     with jax.named_scope("cornerwait"):
         for one in corner_copies:
-            one.wait()
+            one.wait_recv()
     for f in range(6):
         ends = None
         for i in range(8):
@@ -377,6 +403,9 @@
             )
             result.append([finish(sr(k, t), sk(k, t), u[k][t], corr[k])[0:ny] for k in range(3)])
         ends.append(result)
+    with jax.named_scope("sendwait"):
+        for one in x_copies + z_copies + corner_copies:
+            one.wait_send()
     for t in range(tiles):
         for k in range(3):
             w[k, t] = jnp.where(left, ends[0][t][k], ends[1][t][k])

time: 18.7 us -> 15.9 us (0.85)
  the two profiles are of different devices: /device:TPU:0 before, /device:TPU:11 now
where the time goes in v2:
time: 15.9 us; the launch traced here: 15.8 us
  Pallas kernels  15.1 us (95%)
  local copies, waits for them, and re-layouts  0.68 us (4%)
    pallas_call x1, Pallas kernels, on_device(): pl.pallas_call(functools.partial(kernel, sizes, nx, ny, nz), out_shape=pl...  15.1 us
    unnamed x1, local copies, waits for them, and re-layouts  0.68 us

profile of v2, /device:TPU:11, one launch (start us, length us, event | category | flops | bytes accessed | tf_op | source)
XLA Modules:
  0.0 15.8 jit_solution(3882804633632691431)
XLA Ops:
  0.0 15.1 %shard_map.55 = f32[3,8,16,128]{3,2,1,0:T(8,128)S(1)} custom-call(f32[8]{0:T(128)} %cond_hbm.1, f32[3,8,16,128]{3,2,1,0:T(8,128)} %rhs_hbm.1, f32[3,8,16,128]{3,2,1,0:T(8,128)} %frac_hbm.1, s32[8,16,128]{2,1,0:T(8,128)} %reg_hbm.1, s32[3,8,16,128]{3,2,1,0:T(8,128)} %flag_hbm.1), custom_call_target="tpu_custom_call" | custom-call | tf_op jit(solution)/shard_map/pallas_call | solution.py:462
  15.1 0.7 %copy.7 = f32[3,8,16,128]{3,2,1,0:T(8,128)} copy(f32[3,8,16,128]{3,2,1,0:T(8,128)S(1)} %shard_map.55) | data formatting | bytes 393216

commit v3 on v1

v3 whole, which is shorter than its diff:
```python
import functools

import jax
import jax.numpy as jnp
from jax import lax
from jax.experimental import pallas as pl
from jax.experimental.pallas import tpu as pltpu
from jax.sharding import PartitionSpec as P

damping = 0.8
c_node = 0.8 / 7.0
MESH = pl.DeviceIdType.MESH
PAD = 2
SEG = 16


def rot(v, shift, axis):
    return pltpu.roll(v, shift % v.shape[axis], axis)


def y_up(v):
    return rot(v, -1, 0)


def y_down(v):
    return rot(v, 1, 0)


def z_up(v):
    return rot(v, -1, 1)


def z_down(v):
    return rot(v, 1, 1)


def face_zero(u1, u2):
    return (y_up(u2) - u2) - (z_up(u1) - u1)


def face_one(u0, u2, u2p):
    return (z_up(u0) - u0) - (u2p - u2)


def face_two(u0, u1, u1p):
    return (u1p - u1) - (y_up(u0) - u0)


def edges(f0, f1, f2, f1m, f2m):
    return (
        (z_down(f1) - f1) - (y_down(f2) - f2),
        (f2m - f2) - (z_down(f0) - f0),
        (y_down(f0) - f0) - (f1m - f1),
    )


def jacobi_scale(ks):
    return damping / jnp.where(ks > 0.0, 4.0 + ks, 1.0)


def start_iter(rhs, ks):
    return jnp.where(ks > 0.0, jacobi_scale(ks) * rhs, 0.0)


def next_iter(rhs, ks, u, cc):
    new = u + jacobi_scale(ks) * (rhs - (cc + ks * u))
    return jnp.where(ks > 0.0, new, 0.0)


def masked_residual(rhs, ks, u, cc):
    return jnp.where(ks > 0.0, rhs - (cc + ks * u), 0.0)


def nodal_rhs(m0, m0m, m1, m2):
    m1m, m2m = y_down(m1), z_down(m2)
    return (
        (m0m - m0) + (m1m - m1) + (m2m - m2),
        (m0 + m0m) * 0.5,
        (m1 + m1m) * 0.5,
        (m2 + m2m) * 0.5,
    )


def nodal_step(r, rm, rp):
    around = (rm + rp) + (y_up(r) + y_down(r)) + (z_up(r) + z_down(r))
    return (1.2 * c_node) * r + (c_node * c_node) * around


def finish(rhs, ks, u, corr):
    fixed = damping * rhs
    fixed = fixed + damping * (rhs - fixed)
    return jnp.where(ks > 0.0, u + corr, fixed)


def kernel(
    sizes, nx, ny, nz, cond_hbm, rhs_hbm, frac_hbm, reg_hbm, flag_hbm, out_ref,
    cond, frac_ref, reg_ref, flag_ref,
    e, st, sw, u1, u2, mm, rr, zs, zr, ds, dr, ends_out, ends_in, lower_out, lower_in, upper_out, upper_in,
    ya_out, ya_in, yb_out, yb_in, yc_out, yc_in, yd_out, yd_in, ye_out, ye_in, yf_out, yf_in,
    load, send, recv, near,
):
    gx, gy, gz = sizes
    pos = {"gx": lax.axis_index("gx"), "gy": lax.axis_index("gy"), "gz": lax.axis_index("gz")}
    size = {"gx": gx, "gy": gy, "gz": gz}
    first, last = PAD, PAD + nx - 1
    scope = jax.named_scope

    def device(**steps):
        return {axis: lax.rem(pos[axis] + (step + size[axis]), size[axis]) for axis, step in steps.items()}

    partners = [device(gx=1), device(gx=-1), device(gy=1)]
    if gy > 2:
        partners.append(device(gy=-1))
    steps = [(x, z) for z in (1, -1) for x in (0, 1, -1)]
    far = [device(gx=x, gz=z) for x, z in steps]
    alternate = gz % 2 == 0
    early = lax.rem(pos["gz"], 2) == 0
    barrier = pltpu.get_barrier_semaphore()

    def greet(devices):
        for one in devices:
            pl.semaphore_signal(barrier, inc=1, device_id=one, device_id_type=MESH)

    greet(partners)
    if alternate:
        pl.when(early)(lambda: greet(far))
    else:
        greet(far)
    own_rows = pl.ds(0, ny)
    loads = [
        pltpu.make_async_copy(src, dst, load.at[i])
        for i, (src, dst) in enumerate(
            (
                (cond_hbm, cond), (reg_hbm, reg_ref), (frac_hbm, frac_ref), (flag_hbm, flag_ref),
                (rhs_hbm, e.at[pl.ds(0, 3), pl.ds(first, nx), own_rows]),
            )
        )
    ]
    with scope("load"):
        for one in loads:
            one.start()
        for one in loads:
            one.wait()

    started = []
    numbers = iter(range(64))

    def copy(src, dst, where, start=True):
        number = next(numbers)
        made = pltpu.make_async_remote_copy(
            src_ref=src, dst_ref=dst, send_sem=send.at[number], recv_sem=recv.at[number],
            device_id=where, device_id_type=MESH,
        )
        started.append(made)
        if start:
            made.start()
        return made

    row = lax.broadcasted_iota(jnp.int32, (8, nz), 0)
    top, bottom, halo = slice(0, 8), slice(ny - 8, ny), slice(ny, ny + 8)

    def y_start(places, out, into):
        for i, (ref, where) in enumerate(places):
            out[i] = jnp.where(row < 4, ref[(*where, top, slice(None))], ref[(*where, bottom, slice(None))])
        if gy == 2:
            return [copy(out, into.at[0], device(gy=1))]
        return [copy(out, into.at[0], device(gy=-1)), copy(out, into.at[1], device(gy=1))]

    def y_finish(copies, places, into):
        for one in copies:
            one.wait_recv()
        for i, (ref, where) in enumerate(places):
            tile = into[0, i] if gy == 2 else jnp.where(row < 4, into[0, i], into[1, i])
            ref[(*where, halo, slice(None))] = tile

    lane = lax.broadcasted_iota(jnp.int32, (ny, nz), 1)
    slot = lane // SEG
    half = nz // 2
    low_half = lane < half
    quad = (lane % SEG) // 4
    left = (lane % SEG) < 8

    def end_piece(v, j):
        return rot(v, 8 + SEG * j, 1)

    def pick(base, where, other):
        return other if base is None else jnp.where(where, other, base)

    packs = [None] * 6
    with scope("pack"):
        for x in range(nx):
            region = reg_ref[x]
            sigma = jnp.zeros((ny, nz), jnp.float32)
            for number in range(cond.shape[0]):
                sigma = jnp.where(region == number, cond[number], sigma)
            for k in range(3):
                ks = jnp.where(flag_ref[k, x] == 0, sigma * frac_ref[k, x], 0.0)
                e[3 + k, first + x, 0:ny, :] = ks
                for f, v in ((k, e[k, first + x, 0:ny, :]), (3 + k, ks)):
                    packs[f] = pick(packs[f], slot == x, end_piece(v, x))
        for side, off in ((0, 8), (1, 4)):
            tiles = [None, None]
            for f in range(6):
                tiles[f // 4] = pick(tiles[f // 4], quad == f % 4, rot(packs[f], 4 * (f % 4) - off, 1))
            for i in range(2):
                zs[side, i] = tiles[i]
            other = rot(tiles[1], half, 1)
            ds[0, side] = jnp.where(low_half, other, tiles[0])
            ds[1, side] = jnp.where(low_half, tiles[0], other)
        starts = [start_iter(packs[k], packs[3 + k]) for k in range(3)]
        moves = (
            [(f, packs[f], 1, 2 * f, 2) for f in range(6)] + [(k, starts[k], 3, 11 + k, 1) for k in (1, 2)],
            [(f, packs[f], nx - 2, 2 * f, 2) for f in range(6)] + [(k, starts[k], nx - 3, 12 + k, 1) for k in range(3)],
        )
        for side in range(2):
            tiles = [None, None]
            for f, v, at, to, wide in moves[side]:
                t, to = divmod(to, 8)
                tiles[t] = pick(tiles[t], (slot >= to) & (slot < to + wide), rot(v, SEG * (to - at), 1))
            for i in range(2):
                ends_out[side, i] = tiles[i]

    with scope("barrierwait"):
        if alternate:
            pl.semaphore_wait(barrier, jnp.where(early, len(partners), len(partners) + len(far)))

            @pl.when(jnp.logical_not(early))
            def _():
                for i, (x, z) in enumerate(steps):
                    there = steps.index((-x, -z))
                    pl.semaphore_signal(near.at[there], inc=1, device_id=far[i], device_id_type=MESH)
        else:
            pl.semaphore_wait(barrier, len(partners) + len(far))

    own = [(e, (f, p)) for f in range(6) for p in range(first, last + 1)]
    y_own = y_start(own, ya_out, ya_in)

    up, down = device(gx=1), device(gx=-1)
    ends_copies = [copy(ends_out.at[0], ends_in.at[0], down, False), copy(ends_out.at[1], ends_in.at[1], up, False)]
    raw_copies = [
        copy(e.at[:, first, own_rows], e.at[:, last + 1, own_rows], down, False),
        copy(e.at[:, last, own_rows], e.at[:, first - 1, own_rows], up, False),
    ]
    late_copies = [
        copy(upper_out, upper_in.at[:, own_rows], down, False),
        copy(lower_out, lower_in.at[:, own_rows], up, False),
    ]
    z_copies = [copy(zs.at[0], zr.at[0], device(gz=-1), False), copy(zs.at[1], zr.at[1], device(gz=1), False)]
    corner_copies = [
        copy(ds.at[side, zside], dr.at[side, zside], device(gx=1 - 2 * side, gz=2 * zside - 1), False)
        for side in range(2) for zside in range(2)
    ]

    def start(*copies):
        for one in copies:
            one.start()

    def start_far():
        start(*corner_copies, *z_copies)

    up_first = lax.rem(pos["gx"], 4) == 3

    def in_order(begin):
        pl.when(up_first)(lambda: begin(1, 0))
        pl.when(jnp.logical_not(up_first))(lambda: begin(0, 1))

    if alternate:
        pl.when(jnp.logical_not(early))(start_far)
    else:
        start_far()
    in_order(lambda a, b: start(ends_copies[a], raw_copies[a], ends_copies[b]))

    def faces(u, p):
        v0, v1, v2 = u[0, p], u[1, p], u[2, p]
        return face_one(v0, v2, u[2, p + 1]), face_two(v0, v1, u[1, p + 1])

    def curl_sweep(u, before, lo, hi, emit, after=None):
        f1m, f2m = before
        for p in range(lo, hi):
            f1, f2 = faces(u, p) if after is None or p < hi - 1 else after
            f0 = face_zero(u[1, p], u[2, p])
            cc = edges(f0, f1, f2, f1m, f2m)
            for k in range(3):
                emit(k, p, cc[k])
            f1m, f2m = f1, f2

    def emit_second(k, p, cc):
        u2[k, p] = next_iter(e[k, p], e[3 + k, p], u1[k, p], cc)

    def emit_masked(k, p, cc):
        mm[k, p] = masked_residual(e[k, p], e[3 + k, p], u2[k, p], cc)

    def emit_rest(k, p, cc):
        if k > 0 or p != first + 1:
            emit_masked(k, p, cc)

    def node_range(lo, hi):
        for p in range(lo, hi):
            r = nodal_rhs(mm[0, p], mm[0, p - 1], mm[1, p], mm[2, p])
            for q in range(4):
                rr[q, p] = r[q]

    def first_range(lo, hi):
        for p in range(lo, hi):
            for k in range(3):
                u1[k, p] = start_iter(e[k, p], e[3 + k, p])

    def below(v, p):
        up0 = v[0, p]
        return (z_up(up0) - up0) + v[2, p], v[1, p] + (y_up(up0) - up0)

    with scope("y1"):
        y_finish(y_own, own, ya_in)
    with scope("inner"):
        first_range(first, last + 1)
        curl_sweep(u1, faces(u1, first), first + 1, last, emit_second)
        p = last - 1
        sent = (*below(u1, p), e[3, p], *below(u2, p), e[0, p] - e[3, p] * u2[0, p])
        for i, v in enumerate(sent):
            lower_out[i] = v[0:ny]
        p = first + 1
        f1, f2 = faces(u2, p)
        cc = edges(face_zero(u2[1, p], u2[2, p]), f1, f2, -u2[2, p], u2[1, p])
        m0, m1, m2 = [masked_residual(e[k, p], e[3 + k, p], u2[k, p], cc[k]) for k in range(3)]
        mm[0, p] = m0
        sent = (u1[1, p], u1[2, p], e[4, p], e[5, p], u2[1, p], u2[2, p], m0, (y_down(m1) - m1) + (z_down(m2) - m2))
        for i, v in enumerate(sent):
            upper_out[i] = v[0:ny]
    in_order(lambda a, b: start(late_copies[a], raw_copies[b], late_copies[b]))
    with scope("inner2"):
        curl_sweep(u2, faces(u2, first + 1), first + 2, last - 1, emit_masked)
        node_range(first + 2, last - 1)

    with scope("nearwait"):
        if alternate:
            @pl.when(early)
            def _():
                for i in range(len(steps)):
                    pl.semaphore_wait(near.at[i], 1)
                start_far()

    def relay(name, copies, places, out, into):
        with scope(name):
            for one in copies:
                one.wait_recv()
            return y_start(places, out, into)

    raw_up = [(e, (f, last + 1)) for f in range(6)]
    raw_low = [(e, (f, first - 1)) for f in range(6)]
    late_up = [(upper_in, (i,)) for i in range(6)]
    late_low = [(lower_in, (i,)) for i in range(6)]
    strip_tiles = [(st, (f, t)) for f in range(6) for t in range(4)]
    y_raw_up = relay("rawup", raw_copies[:1], raw_up, yb_out, yb_in)
    y_late_up = relay("lateup", late_copies[:1], late_up, yc_out, yc_in)

    with scope("endswait"):
        for one in ends_copies + z_copies + corner_copies:
            one.wait_recv()
    with scope("strippack"):
        for f in range(6):
            t, to = divmod(2 * f, 8)
            piece = rot(ends_in[0, t], SEG * (1 - to), 1)
            piece = jnp.where(slot == 0, end_piece(e[f, last + 1, 0:ny, :], 0), piece)
            piece = jnp.where(slot >= nx - 2, rot(ends_in[1, t], SEG * (nx - 2 - to), 1), piece)
            if f < 3:
                piece = jnp.where(slot == 3, rot(ends_in[0, 1], SEG * (3 - (3 + f)), 1), piece)
                piece = jnp.where(slot == nx - 3, rot(ends_in[1, 1], SEG * (nx - 3 - (4 + f)), 1), piece)
            corner = []
            for zside, off in ((0, 8), (1, 4)):
                plus, minus = dr[1, zside], dr[0, zside]
                if f < 4:
                    corner.append(rot(jnp.where(low_half, plus, minus), off - 4 * f, 1))
                else:
                    corner.append(rot(jnp.where(low_half, minus, plus), half + off - 4 * (f - 4), 1))
            mid = packs[f]
            st[f, 0, 0:ny, :] = jnp.where(left, mid, rot(zr[0, f // 4], 8 - 4 * (f % 4), 1))
            st[f, 1, 0:ny, :] = jnp.where(left, piece, corner[0])
            st[f, 2, 0:ny, :] = jnp.where(left, rot(zr[1, f // 4], 4 - 4 * (f % 4), 1), mid)
            st[f, 3, 0:ny, :] = jnp.where(left, corner[1], piece)
        y_strip = y_start(strip_tiles, yd_out, yd_in)

    y_raw_low = relay("rawlow", raw_copies[1:], raw_low, ye_out, ye_in)

    inner = (lane >= 4) & (lane < nz - 4)

    def node_at(p, count=4):
        return [nodal_step(rr[q, p], rr[q, p - 1], rr[q, p + 1]) for q in range(count)]

    def outputs(lo, hi, kept):
        s_next = node_at(lo)
        for p in range(lo, hi):
            s = s_next
            s_next = node_at(p + 1, 4 if p + 1 < hi else 2)
            corr = (
                (s_next[0] - s[0]) + (s[1] + s_next[1]) * 0.5,
                (y_up(s[0]) - s[0]) + (s[2] + y_up(s[2])) * 0.5,
                (z_up(s[0]) - s[0]) + (s[3] + z_up(s[3])) * 0.5,
            )
            for k in range(3):
                body = finish(e[k, p, 0:ny], e[3 + k, p, 0:ny], u2[k, p, 0:ny], corr[k][0:ny])
                ends = rot(sw[k], nz - 8 - SEG * (p - first), 1)
                out_ref[k, p - first] = jnp.where(inner, body, ends)

    lane24 = lax.broadcasted_iota(jnp.int32, (ny + 8, nz), 1)
    slot24 = lane24 // SEG
    left24 = (lane24 % SEG) < 8

    def x_up(vs):
        rs = [rot(v, -SEG, 1) for v in vs]
        return [jnp.where(lane24 < nz - SEG, rs[t], rs[(t + 1) % len(rs)]) for t in range(len(rs))]

    def x_down(vs):
        rs = [rot(v, SEG, 1) for v in vs]
        return [jnp.where(lane24 >= SEG, rs[t], rs[t - 1]) for t in range(len(rs))]

    span = range(2)

    def strip_curl(u):
        u1p, u2p = x_up(u[1]), x_up(u[2])
        f0 = [face_zero(u[1][t], u[2][t]) for t in span]
        f1 = [face_one(u[0][t], u[2][t], u2p[t]) for t in span]
        f2 = [face_two(u[0][t], u[1][t], u1p[t]) for t in span]
        f1m, f2m = x_down(f1), x_down(f2)
        out = [edges(f0[t], f1[t], f2[t], f1m[t], f2m[t]) for t in span]
        return [[out[t][k] for t in span] for k in range(3)]

    def strips():
        results = []
        for base in (0, 2):
            def sr(k, t):
                return st[k, base + t]

            def sk(k, t):
                return st[3 + k, base + t]

            sent = ((slot24 == 3) | (slot24 == nx - 3)) & (left24 if base == 0 else ~left24)
            u = [[start_iter(sr(k, t), sk(k, t)) for t in span] for k in range(3)]
            for k in range(3):
                u[k][1] = jnp.where(sent, sr(k, 1), u[k][1])
            cc = strip_curl(u)
            u = [[next_iter(sr(k, t), sk(k, t), u[k][t], cc[k][t]) for t in span] for k in range(3)]
            cc = strip_curl(u)
            m = [[masked_residual(sr(k, t), sk(k, t), u[k][t], cc[k][t]) for t in span] for k in range(3)]
            m0m = x_down(m[0])
            r = [nodal_rhs(m[0][t], m0m[t], m[1][t], m[2][t]) for t in span]
            s = []
            for q in range(4):
                rq = [r[t][q] for t in span]
                rm, rp = x_down(rq), x_up(rq)
                s.append([nodal_step(rq[t], rm[t], rp[t]) for t in span])
            s0p, s1p = x_up(s[0])[0], x_up(s[1])[0]
            s0, s1, s2, s3 = [s[q][0] for q in range(4)]
            corr = (
                (s0p - s0) + (s1 + s1p) * 0.5,
                (y_up(s0) - s0) + (s2 + y_up(s2)) * 0.5,
                (z_up(s0) - s0) + (s3 + z_up(s3)) * 0.5,
            )
            results.append([finish(sr(k, 0), sk(k, 0), u[k][0], corr[k])[0:ny] for k in range(3)])
        for k in range(3):
            sw[k] = jnp.where(left, results[0][k], results[1][k])

    with scope("yup"):
        y_finish(y_raw_up, raw_up, yb_in)
        y_finish(y_late_up, late_up, yc_in)
    with scope("upper"):
        p = last + 1
        first_range(p, p + 1)
        f1 = face_one(u1[0, p], u1[2, p], upper_in[1])
        f2 = face_two(u1[0, p], u1[1, p], upper_in[0])
        curl_sweep(u1, faces(u1, last - 1), last, p + 1, emit_second, (f1, f2))
        f1 = face_one(u2[0, p], u2[2, p], upper_in[5])
        f2 = face_two(u2[0, p], u2[1, p], upper_in[4])
        curl_sweep(u2, faces(u2, last - 2), last - 1, p + 1, emit_masked, (f1, f2))
        node_range(last - 1, p + 1)
        v0 = u2[0, p]
        q2 = jnp.where(upper_in[2] > 0.0, u2[1, p] + (y_up(v0) - v0), 0.0)
        q1 = jnp.where(upper_in[3] > 0.0, (z_up(v0) - v0) + u2[2, p], 0.0)
        m0, m0p = mm[0, p], upper_in[6]
        rr[0, p + 1] = (m0 - m0p) + (upper_in[7] + (y_down(q2) - q2) + (z_down(q1) - q1))
        rr[1, p + 1] = (m0p + m0) * 0.5

    with scope("ystrip"):
        y_finish(y_strip, strip_tiles, yd_in)
    with scope("strips"):
        strips()
    with scope("outup"):
        outputs(first + 3, last + 1, None)
    y_late_low = relay("latelow", late_copies[1:], late_low, yf_out, yf_in)
    with scope("ylow"):
        y_finish(y_raw_low, raw_low, ye_in)
        y_finish(y_late_low, late_low, yf_in)
    with scope("lower"):
        p = first - 1
        first_range(p, p + 1)
        curl_sweep(u1, (lower_in[0] - u1[2, p], u1[1, p] - lower_in[1]), p, first + 1, emit_second)
        f1, f2 = lower_in[3] - u2[2, p], u2[1, p] - lower_in[4]
        cc = (z_down(f1) - f1) - (y_down(f2) - f2)
        mm[0, p - 1] = jnp.where(lower_in[2] > 0.0, lower_in[5] - cc, 0.0)
        curl_sweep(u2, (f1, f2), p, first + 2, emit_rest)
        node_range(p, first + 2)
    with scope("outlow"):
        outputs(first, first + 3, None)
    with scope("sendwait"):
        for one in started:
            one.wait_send()


def on_device(sizes, rhs, conductivity, fraction, region, flags):
    _, nx, ny, nz = rhs.shape
    planes = nx + 2 * PAD
    rows = ny + 8
    f32 = jnp.float32
    hbm = pl.BlockSpec(memory_space=pl.ANY)
    sides = 1 if sizes[1] == 2 else 2
    relays = []
    for count in (6 * nx, 6, 6, 24, 6, 6):
        relays += [pltpu.VMEM((count, 8, nz), f32), pltpu.VMEM((sides, count, 8, nz), f32)]
    return pl.pallas_call(
        functools.partial(kernel, sizes, nx, ny, nz),
        out_shape=pltpu.VMEM(rhs.shape, rhs.dtype),
        in_specs=[hbm] * 5,
        out_specs=pl.BlockSpec(memory_space=pltpu.VMEM),
        scratch_shapes=[
            pltpu.SMEM(conductivity.shape, f32),
            pltpu.VMEM(rhs.shape, f32),
            pltpu.VMEM(region.shape, jnp.int32),
            pltpu.VMEM(flags.shape, jnp.int32),
            pltpu.VMEM((6, planes, rows, nz), f32),
            pltpu.VMEM((6, 4, rows, nz), f32),
            pltpu.VMEM((3, ny, nz), f32),
            pltpu.VMEM((3, planes, rows, nz), f32),
            pltpu.VMEM((3, planes, rows, nz), f32),
            pltpu.VMEM((3, planes, rows, nz), f32),
            pltpu.VMEM((4, planes, rows, nz), f32),
            pltpu.VMEM((2, 2, ny, nz), f32),
            pltpu.VMEM((2, 2, ny, nz), f32),
            pltpu.VMEM((2, 2, ny, nz), f32),
            pltpu.VMEM((2, 2, ny, nz), f32),
            pltpu.VMEM((2, 2, ny, nz), f32),
            pltpu.VMEM((2, 2, ny, nz), f32),
            pltpu.VMEM((6, ny, nz), f32),
            pltpu.VMEM((6, rows, nz), f32),
            pltpu.VMEM((8, ny, nz), f32),
            pltpu.VMEM((8, rows, nz), f32),
            *relays,
            pltpu.SemaphoreType.DMA((5,)),
            pltpu.SemaphoreType.DMA((26,)),
            pltpu.SemaphoreType.DMA((26,)),
            pltpu.SemaphoreType.REGULAR((6,)),
        ],
        compiler_params=pltpu.CompilerParams(
            collective_id=0, has_side_effects=True, vmem_limit_bytes=60 * 1024 * 1024
        ),
    )(conductivity, rhs, fraction, region, flags)


def solution(mesh):
    sizes = tuple(mesh.shape[name] for name in ("gx", "gy", "gz"))
    return jax.shard_map(
        functools.partial(on_device, sizes),
        mesh=mesh,
        in_specs=(
            P(None, "gx", "gy", "gz"),
            P(),
            P(None, "gx", "gy", "gz"),
            P("gx", "gy", "gz"),
            P(None, "gx", "gy", "gz"),
        ),
        out_specs=P(None, "gx", "gy", "gz"),
        check_vma=False,
    )
```

time: 18.7 us -> 15.3 us (0.82)
  the two profiles are of different devices: /device:TPU:0 before, /device:TPU:29 now
where the time goes in v3:
time: 15.3 us; the launch traced here: 15.1 us
  Pallas kernels  14.4 us (94%)
  local copies, waits for them, and re-layouts  0.68 us (4%)
    pallas_call x1, Pallas kernels, on_device(): pl.pallas_call(functools.partial(kernel, sizes, nx, ny, nz), out_shape=pl...  14.4 us
    unnamed x1, local copies, waits for them, and re-layouts  0.68 us

profile of v3, /device:TPU:29, one launch (start us, length us, event | category | flops | bytes accessed | tf_op | source)
XLA Modules:
  0.0 15.1 jit_solution(6519423880932720427)
XLA Ops:
  0.0 14.4 %shard_map.55 = f32[3,8,16,128]{3,2,1,0:T(8,128)S(1)} custom-call(f32[8]{0:T(128)} %cond_hbm.1, f32[3,8,16,128]{3,2,1,0:T(8,128)} %rhs_hbm.1, f32[3,8,16,128]{3,2,1,0:T(8,128)} %frac_hbm.1, s32[8,16,128]{2,1,0:T(8,128)} %reg_hbm.1, s32[3,8,16,128]{3,2,1,0:T(8,128)} %flag_hbm.1), custom_call_target="tpu_custom_call" | custom-call | tf_op jit(solution)/shard_map/pallas_call | solution.py:518
  14.4 0.7 %copy.7 = f32[3,8,16,128]{3,2,1,0:T(8,128)} copy(f32[3,8,16,128]{3,2,1,0:T(8,128)S(1)} %shard_map.55) | data formatting | bytes 393216

commit v4 on v3

--- a/solution.py
+++ b/solution.py
@@ -1,4 +1,5 @@
 import functools
+import math
 
 import jax
 import jax.numpy as jnp
@@ -97,7 +98,7 @@
     cond, frac_ref, reg_ref, flag_ref,
     e, st, sw, u1, u2, mm, rr, zs, zr, ds, dr, ends_out, ends_in, lower_out, lower_in, upper_out, upper_in,
     ya_out, ya_in, yb_out, yb_in, yc_out, yc_in, yd_out, yd_in, ye_out, ye_in, yf_out, yf_in,
-    load, send, recv, near,
+    blank, load, send, recv, near,
 ):
     gx, gy, gz = sizes
     pos = {"gx": lax.axis_index("gx"), "gy": lax.axis_index("gy"), "gz": lax.axis_index("gz")}
@@ -129,46 +130,53 @@
     own_rows = pl.ds(0, ny)
     loads = [
         pltpu.make_async_copy(src, dst, load.at[i])
-        for i, (src, dst) in enumerate(
-            (
-                (cond_hbm, cond), (reg_hbm, reg_ref), (frac_hbm, frac_ref), (flag_hbm, flag_ref),
-                (rhs_hbm, e.at[pl.ds(0, 3), pl.ds(first, nx), own_rows]),
-            )
+        for src, dst, i in (
+            (rhs_hbm, e.at[pl.ds(0, 3), pl.ds(first, nx), own_rows], 0), (reg_hbm, reg_ref, 0),
+            (frac_hbm, frac_ref, 0), (flag_hbm, flag_ref, 0), (cond_hbm, cond, 1),
         )
     ]
+
+    def tiles_of(count):
+        return blank.at[pl.ds(0, count)]
+
+    def wait_tiles(semaphore, count):
+        pltpu.make_async_copy(tiles_of(count), tiles_of(count), semaphore).wait()
+
     with scope("load"):
         for one in loads:
             one.start()
-        for one in loads:
-            one.wait()
-
-    started = []
-    numbers = iter(range(64))
-
-    def copy(src, dst, where, start=True):
-        number = next(numbers)
+        loads[4].wait()
+        wait_tiles(load.at[0], 10 * nx * ny // 8)
+
+    sent_tiles = []
+
+    def copy(group, src, dst, where, start=True):
         made = pltpu.make_async_remote_copy(
-            src_ref=src, dst_ref=dst, send_sem=send.at[number], recv_sem=recv.at[number],
+            src_ref=src, dst_ref=dst, send_sem=send.at[0], recv_sem=recv.at[group],
             device_id=where, device_id_type=MESH,
         )
-        started.append(made)
+        sent_tiles.append(math.prod(src.shape) // (8 * nz))
         if start:
             made.start()
         return made
 
+    def arrived(group, count):
+        wait_tiles(recv.at[group], count)
+
     row = lax.broadcasted_iota(jnp.int32, (8, nz), 0)
     top, bottom, halo = slice(0, 8), slice(ny - 8, ny), slice(ny, ny + 8)
 
-    def y_start(places, out, into):
+    def y_start(group, places, out, into):
         for i, (ref, where) in enumerate(places):
             out[i] = jnp.where(row < 4, ref[(*where, top, slice(None))], ref[(*where, bottom, slice(None))])
         if gy == 2:
-            return [copy(out, into.at[0], device(gy=1))]
-        return [copy(out, into.at[0], device(gy=-1)), copy(out, into.at[1], device(gy=1))]
-
-    def y_finish(copies, places, into):
-        for one in copies:
-            one.wait_recv()
+            copy(group, out, into.at[0], device(gy=1))
+        else:
+            copy(group, out, into.at[0], device(gy=-1))
+            copy(group, out, into.at[1], device(gy=1))
+
+    def y_finish(group, places, into):
+        arrived(group, into.shape[0] * len(places))
         for i, (ref, where) in enumerate(places):
             tile = into[0, i] if gy == 2 else jnp.where(row < 4, into[0, i], into[1, i])
             ref[(*where, halo, slice(None))] = tile
@@ -226,28 +234,27 @@
 
             @pl.when(jnp.logical_not(early))
             def _():
-                for i, (x, z) in enumerate(steps):
-                    there = steps.index((-x, -z))
-                    pl.semaphore_signal(near.at[there], inc=1, device_id=far[i], device_id_type=MESH)
+                for one, (_, z) in zip(far, steps):
+                    pl.semaphore_signal(near.at[int(z < 0)], inc=1, device_id=one, device_id_type=MESH)
         else:
             pl.semaphore_wait(barrier, len(partners) + len(far))
 
     own = [(e, (f, p)) for f in range(6) for p in range(first, last + 1)]
-    y_own = y_start(own, ya_out, ya_in)
+    y_start(0, own, ya_out, ya_in)
 
     up, down = device(gx=1), device(gx=-1)
-    ends_copies = [copy(ends_out.at[0], ends_in.at[0], down, False), copy(ends_out.at[1], ends_in.at[1], up, False)]
+    ends_copies = [copy(1, ends_out.at[0], ends_in.at[0], down, False), copy(1, ends_out.at[1], ends_in.at[1], up, False)]
     raw_copies = [
-        copy(e.at[:, first, own_rows], e.at[:, last + 1, own_rows], down, False),
-        copy(e.at[:, last, own_rows], e.at[:, first - 1, own_rows], up, False),
+        copy(2, e.at[:, first, own_rows], e.at[:, last + 1, own_rows], down, False),
+        copy(3, e.at[:, last, own_rows], e.at[:, first - 1, own_rows], up, False),
     ]
     late_copies = [
-        copy(upper_out, upper_in.at[:, own_rows], down, False),
-        copy(lower_out, lower_in.at[:, own_rows], up, False),
+        copy(4, upper_out, upper_in.at[:, own_rows], down, False),
+        copy(5, lower_out, lower_in.at[:, own_rows], up, False),
     ]
-    z_copies = [copy(zs.at[0], zr.at[0], device(gz=-1), False), copy(zs.at[1], zr.at[1], device(gz=1), False)]
+    z_copies = [copy(1, zs.at[0], zr.at[0], device(gz=-1), False), copy(1, zs.at[1], zr.at[1], device(gz=1), False)]
     corner_copies = [
-        copy(ds.at[side, zside], dr.at[side, zside], device(gx=1 - 2 * side, gz=2 * zside - 1), False)
+        copy(1, ds.at[side, zside], dr.at[side, zside], device(gx=1 - 2 * side, gz=2 * zside - 1), False)
         for side in range(2) for zside in range(2)
     ]
 
@@ -255,19 +262,23 @@
         for one in copies:
             one.start()
 
-    def start_far():
-        start(*corner_copies, *z_copies)
-
-    up_first = lax.rem(pos["gx"], 4) == 3
+    def start_far(zside):
+        start(corner_copies[zside], corner_copies[2 + zside], z_copies[zside])
+
+    def start_both():
+        start_far(1)
+        start_far(0)
+
+    up_first = (lax.rem(pos["gx"], 4) == 3) & (pos["gz"] == 0)
 
     def in_order(begin):
         pl.when(up_first)(lambda: begin(1, 0))
         pl.when(jnp.logical_not(up_first))(lambda: begin(0, 1))
 
     if alternate:
-        pl.when(jnp.logical_not(early))(start_far)
+        pl.when(jnp.logical_not(early))(start_both)
     else:
-        start_far()
+        start_both()
     in_order(lambda a, b: start(ends_copies[a], raw_copies[a], ends_copies[b]))
 
     def faces(u, p):
@@ -310,7 +321,7 @@
         return (z_up(up0) - up0) + v[2, p], v[1, p] + (y_up(up0) - up0)
 
     with scope("y1"):
-        y_finish(y_own, own, ya_in)
+        y_finish(0, own, ya_in)
     with scope("inner"):
         first_range(first, last + 1)
         curl_sweep(u1, faces(u1, first), first + 1, last, emit_second)
@@ -326,7 +337,14 @@
         sent = (u1[1, p], u1[2, p], e[4, p], e[5, p], u2[1, p], u2[2, p], m0, (y_down(m1) - m1) + (z_down(m2) - m2))
         for i, v in enumerate(sent):
             upper_out[i] = v[0:ny]
-    in_order(lambda a, b: start(late_copies[a], raw_copies[b], late_copies[b]))
+    @pl.when(up_first)
+    def _():
+        start(raw_copies[0], late_copies[1], late_copies[0])
+
+    @pl.when(jnp.logical_not(up_first))
+    def _():
+        start(late_copies[0], raw_copies[1], late_copies[1])
+
     with scope("inner2"):
         curl_sweep(u2, faces(u2, first + 1), first + 2, last - 1, emit_masked)
         node_range(first + 2, last - 1)
@@ -335,51 +353,22 @@
         if alternate:
             @pl.when(early)
             def _():
-                for i in range(len(steps)):
-                    pl.semaphore_wait(near.at[i], 1)
-                start_far()
-
-    def relay(name, copies, places, out, into):
+                for zside in (1, 0):
+                    pl.semaphore_wait(near.at[zside], len(far) // 2)
+                    start_far(zside)
+
+    def relay(name, group, count, places, out, into):
         with scope(name):
-            for one in copies:
-                one.wait_recv()
-            return y_start(places, out, into)
+            arrived(group, count * ny // 8)
+            y_start(4 + group, places, out, into)
 
     raw_up = [(e, (f, last + 1)) for f in range(6)]
     raw_low = [(e, (f, first - 1)) for f in range(6)]
     late_up = [(upper_in, (i,)) for i in range(6)]
     late_low = [(lower_in, (i,)) for i in range(6)]
     strip_tiles = [(st, (f, t)) for f in range(6) for t in range(4)]
-    y_raw_up = relay("rawup", raw_copies[:1], raw_up, yb_out, yb_in)
-    y_late_up = relay("lateup", late_copies[:1], late_up, yc_out, yc_in)
-
-    with scope("endswait"):
-        for one in ends_copies + z_copies + corner_copies:
-            one.wait_recv()
-    with scope("strippack"):
-        for f in range(6):
-            t, to = divmod(2 * f, 8)
-            piece = rot(ends_in[0, t], SEG * (1 - to), 1)
-            piece = jnp.where(slot == 0, end_piece(e[f, last + 1, 0:ny, :], 0), piece)
-            piece = jnp.where(slot >= nx - 2, rot(ends_in[1, t], SEG * (nx - 2 - to), 1), piece)
-            if f < 3:
-                piece = jnp.where(slot == 3, rot(ends_in[0, 1], SEG * (3 - (3 + f)), 1), piece)
-                piece = jnp.where(slot == nx - 3, rot(ends_in[1, 1], SEG * (nx - 3 - (4 + f)), 1), piece)
-            corner = []
-            for zside, off in ((0, 8), (1, 4)):
-                plus, minus = dr[1, zside], dr[0, zside]
-                if f < 4:
-                    corner.append(rot(jnp.where(low_half, plus, minus), off - 4 * f, 1))
-                else:
-                    corner.append(rot(jnp.where(low_half, minus, plus), half + off - 4 * (f - 4), 1))
-            mid = packs[f]
-            st[f, 0, 0:ny, :] = jnp.where(left, mid, rot(zr[0, f // 4], 8 - 4 * (f % 4), 1))
-            st[f, 1, 0:ny, :] = jnp.where(left, piece, corner[0])
-            st[f, 2, 0:ny, :] = jnp.where(left, rot(zr[1, f // 4], 4 - 4 * (f % 4), 1), mid)
-            st[f, 3, 0:ny, :] = jnp.where(left, corner[1], piece)
-        y_strip = y_start(strip_tiles, yd_out, yd_in)
-
-    y_raw_low = relay("rawlow", raw_copies[1:], raw_low, ye_out, ye_in)
+    relay("rawup", 2, 6, raw_up, yb_out, yb_in)
+    relay("lateup", 4, 8, late_up, yc_out, yc_in)
 
     inner = (lane >= 4) & (lane < nz - 4)
 
@@ -459,9 +448,35 @@
         for k in range(3):
             sw[k] = jnp.where(left, results[0][k], results[1][k])
 
+    relay("rawlow", 3, 6, raw_low, ye_out, ye_in)
+    with scope("endswait"):
+        arrived(1, 12 * ny // 8)
+    with scope("strippack"):
+        for f in range(6):
+            t, to = divmod(2 * f, 8)
+            piece = rot(ends_in[0, t], SEG * (1 - to), 1)
+            piece = jnp.where(slot == 0, end_piece(e[f, last + 1, 0:ny, :], 0), piece)
+            piece = jnp.where(slot >= nx - 2, rot(ends_in[1, t], SEG * (nx - 2 - to), 1), piece)
+            if f < 3:
+                piece = jnp.where(slot == 3, rot(ends_in[0, 1], SEG * (3 - (3 + f)), 1), piece)
+                piece = jnp.where(slot == nx - 3, rot(ends_in[1, 1], SEG * (nx - 3 - (4 + f)), 1), piece)
+            corner = []
+            for zside, off in ((0, 8), (1, 4)):
+                plus, minus = dr[1, zside], dr[0, zside]
+                if f < 4:
+                    corner.append(rot(jnp.where(low_half, plus, minus), off - 4 * f, 1))
+                else:
+                    corner.append(rot(jnp.where(low_half, minus, plus), half + off - 4 * (f - 4), 1))
+            mid = packs[f]
+            st[f, 0, 0:ny, :] = jnp.where(left, mid, rot(zr[0, f // 4], 8 - 4 * (f % 4), 1))
+            st[f, 1, 0:ny, :] = jnp.where(left, piece, corner[0])
+            st[f, 2, 0:ny, :] = jnp.where(left, rot(zr[1, f // 4], 4 - 4 * (f % 4), 1), mid)
+            st[f, 3, 0:ny, :] = jnp.where(left, corner[1], piece)
+        y_start(10, strip_tiles, yd_out, yd_in)
+
     with scope("yup"):
-        y_finish(y_raw_up, raw_up, yb_in)
-        y_finish(y_late_up, late_up, yc_in)
+        y_finish(6, raw_up, yb_in)
+        y_finish(8, late_up, yc_in)
     with scope("upper"):
         p = last + 1
         first_range(p, p + 1)
@@ -479,16 +494,16 @@
         rr[0, p + 1] = (m0 - m0p) + (upper_in[7] + (y_down(q2) - q2) + (z_down(q1) - q1))
         rr[1, p + 1] = (m0p + m0) * 0.5
 
+    relay("latelow", 5, 6, late_low, yf_out, yf_in)
     with scope("ystrip"):
-        y_finish(y_strip, strip_tiles, yd_in)
+        y_finish(10, strip_tiles, yd_in)
     with scope("strips"):
         strips()
     with scope("outup"):
         outputs(first + 3, last + 1, None)
-    y_late_low = relay("latelow", late_copies[1:], late_low, yf_out, yf_in)
     with scope("ylow"):
-        y_finish(y_raw_low, raw_low, ye_in)
-        y_finish(y_late_low, late_low, yf_in)
+        y_finish(7, raw_low, ye_in)
+        y_finish(9, late_low, yf_in)
     with scope("lower"):
         p = first - 1
         first_range(p, p + 1)
@@ -501,8 +516,7 @@
     with scope("outlow"):
         outputs(first, first + 3, None)
     with scope("sendwait"):
-        for one in started:
-            one.wait_send()
+        wait_tiles(send.at[0], sum(sent_tiles))
 
 
 def on_device(sizes, rhs, conductivity, fraction, region, flags):
@@ -543,10 +557,11 @@
             pltpu.VMEM((8, ny, nz), f32),
             pltpu.VMEM((8, rows, nz), f32),
             *relays,
-            pltpu.SemaphoreType.DMA((5,)),
-            pltpu.SemaphoreType.DMA((26,)),
-            pltpu.SemaphoreType.DMA((26,)),
-            pltpu.SemaphoreType.REGULAR((6,)),
+            pltpu.VMEM((320, 8, nz), f32),
+            pltpu.SemaphoreType.DMA((2,)),
+            pltpu.SemaphoreType.DMA((1,)),
+            pltpu.SemaphoreType.DMA((11,)),
+            pltpu.SemaphoreType.REGULAR((2,)),
         ],
         compiler_params=pltpu.CompilerParams(
             collective_id=0, has_side_effects=True, vmem_limit_bytes=60 * 1024 * 1024

time: 15.3 us -> 13.9 us (0.908)
  the two profiles are of different devices: /device:TPU:29 before, /device:TPU:25 now
where the time goes in v4:
time: 13.9 us; the launch traced here: 13.7 us
  Pallas kernels  13 us (94%)
  local copies, waits for them, and re-layouts  0.68 us (5%)
    pallas_call x1, Pallas kernels, on_device(): pl.pallas_call(functools.partial(kernel, sizes, nx, ny, nz), out_shape=pl...  13 us
    unnamed x1, local copies, waits for them, and re-layouts  0.68 us

profile of v4, /device:TPU:25, one launch (start us, length us, event | category | flops | bytes accessed | tf_op | source)
XLA Modules:
  0.0 13.7 jit_solution(2393546426127359827)
XLA Ops:
  0.0 13.0 %shard_map.55 = f32[3,8,16,128]{3,2,1,0:T(8,128)S(1)} custom-call(f32[8]{0:T(128)} %cond_hbm.1, f32[3,8,16,128]{3,2,1,0:T(8,128)} %rhs_hbm.1, f32[3,8,16,128]{3,2,1,0:T(8,128)} %frac_hbm.1, s32[8,16,128]{2,1,0:T(8,128)} %reg_hbm.1, s32[3,8,16,128]{3,2,1,0:T(8,128)} %flag_hbm.1), custom_call_target="tpu_custom_call" | custom-call | tf_op jit(solution)/shard_map/pallas_call | solution.py:532
  13.0 0.7 %copy.7 = f32[3,8,16,128]{3,2,1,0:T(8,128)} copy(f32[3,8,16,128]{3,2,1,0:T(8,128)S(1)} %shard_map.55) | data formatting | bytes 393216

commit v5 on v4

--- a/solution.py
+++ b/solution.py
@@ -97,7 +97,7 @@
     sizes, nx, ny, nz, cond_hbm, rhs_hbm, frac_hbm, reg_hbm, flag_hbm, out_ref,
     cond, frac_ref, reg_ref, flag_ref,
     e, st, sw, u1, u2, mm, rr, zs, zr, ds, dr, ends_out, ends_in, lower_out, lower_in, upper_out, upper_in,
-    ya_out, ya_in, yb_out, yb_in, yc_out, yc_in, yd_out, yd_in, ye_out, ye_in, yf_out, yf_in,
+    ya_out, ya_in, yb_out, yb_in, yc_out, yc_in, yd_out, yd_in,
     blank, load, send, recv, near,
 ):
     gx, gy, gz = sizes
@@ -109,24 +109,23 @@
     def device(**steps):
         return {axis: lax.rem(pos[axis] + (step + size[axis]), size[axis]) for axis, step in steps.items()}
 
-    partners = [device(gx=1), device(gx=-1), device(gy=1)]
-    if gy > 2:
-        partners.append(device(gy=-1))
     steps = [(x, z) for z in (1, -1) for x in (0, 1, -1)]
-    far = [device(gx=x, gz=z) for x, z in steps]
-    alternate = gz % 2 == 0
-    early = lax.rem(pos["gz"], 2) == 0
+    paired = gy == 2
     barrier = pltpu.get_barrier_semaphore()
 
-    def greet(devices):
+    def greet(*devices):
         for one in devices:
             pl.semaphore_signal(barrier, inc=1, device_id=one, device_id_type=MESH)
 
-    greet(partners)
-    if alternate:
-        pl.when(early)(lambda: greet(far))
+    def on(core, **steps):
+        return {**device(**steps), "gy": core}
+
+    if paired:
+        greet(on(1, gx=1), on(1, gx=-1))
+        pl.when(pos["gy"] == 0)(lambda: greet(device(gy=1)))
+        greet(*(on(0, gx=x, gz=z) for x, z in steps))
     else:
-        greet(far)
+        greet(device(gx=1), device(gx=-1), device(gy=1), device(gy=-1), *(device(gx=x, gz=z) for x, z in steps))
     own_rows = pl.ds(0, ny)
     loads = [
         pltpu.make_async_copy(src, dst, load.at[i])
@@ -145,6 +144,14 @@
     with scope("load"):
         for one in loads:
             one.start()
+        if paired:
+            @pl.when(pos["gy"] == 1)
+            def _():
+                pl.semaphore_wait(barrier, 5)
+                pl.semaphore_signal(near.at[0], inc=1, device_id=device(gy=1), device_id_type=MESH)
+        else:
+            pl.semaphore_wait(barrier, 4 + len(steps))
+
         loads[4].wait()
         wait_tiles(load.at[0], 10 * nx * ny // 8)
 
@@ -229,15 +236,23 @@
                 ends_out[side, i] = tiles[i]
 
     with scope("barrierwait"):
-        if alternate:
-            pl.semaphore_wait(barrier, jnp.where(early, len(partners), len(partners) + len(far)))
-
-            @pl.when(jnp.logical_not(early))
+        if paired:
+            @pl.when(pos["gy"] == 0)
             def _():
-                for one, (_, z) in zip(far, steps):
-                    pl.semaphore_signal(near.at[int(z < 0)], inc=1, device_id=one, device_id_type=MESH)
-        else:
-            pl.semaphore_wait(barrier, len(partners) + len(far))
+                pl.semaphore_wait(near.at[0], 1)
+
+    def far_wait():
+        if not paired:
+            return
+
+        @pl.when(pos["gy"] == 0)
+        def _():
+            pl.semaphore_wait(barrier, 2 * len(steps))
+            pl.semaphore_signal(near.at[1], inc=1, device_id=device(gy=1), device_id_type=MESH)
+
+        @pl.when(pos["gy"] == 1)
+        def _():
+            pl.semaphore_wait(near.at[1], 1)
 
     own = [(e, (f, p)) for f in range(6) for p in range(first, last + 1)]
     y_start(0, own, ya_out, ya_in)
@@ -275,11 +290,17 @@
         pl.when(up_first)(lambda: begin(1, 0))
         pl.when(jnp.logical_not(up_first))(lambda: begin(0, 1))
 
-    if alternate:
-        pl.when(jnp.logical_not(early))(start_both)
-    else:
-        start_both()
-    in_order(lambda a, b: start(ends_copies[a], raw_copies[a], ends_copies[b]))
+    late_start = pos["gz"] == 0
+    in_order(lambda a, b: start(ends_copies[a], ends_copies[b]))
+
+    in_order(lambda a, b: start(raw_copies[a]))
+
+    @pl.when(jnp.logical_not(late_start))
+    def _():
+        with scope("nearwait"):
+            far_wait()
+            start_both()
+
 
     def faces(u, p):
         v0, v1, v2 = u[0, p], u[1, p], u[2, p]
@@ -349,26 +370,24 @@
         curl_sweep(u2, faces(u2, first + 1), first + 2, last - 1, emit_masked)
         node_range(first + 2, last - 1)
 
-    with scope("nearwait"):
-        if alternate:
-            @pl.when(early)
-            def _():
-                for zside in (1, 0):
-                    pl.semaphore_wait(near.at[zside], len(far) // 2)
-                    start_far(zside)
-
-    def relay(name, group, count, places, out, into):
+    @pl.when(late_start)
+    def _():
+        with scope("nearwait"):
+            far_wait()
+            start_both()
+
+    def relay(name, groups, places, out, into):
         with scope(name):
-            arrived(group, count * ny // 8)
-            y_start(4 + group, places, out, into)
+            for group, count in groups:
+                arrived(group, count * ny // 8)
+            y_start(4 + groups[0][0], places, out, into)
 
     raw_up = [(e, (f, last + 1)) for f in range(6)]
     raw_low = [(e, (f, first - 1)) for f in range(6)]
     late_up = [(upper_in, (i,)) for i in range(6)]
     late_low = [(lower_in, (i,)) for i in range(6)]
     strip_tiles = [(st, (f, t)) for f in range(6) for t in range(4)]
-    relay("rawup", 2, 6, raw_up, yb_out, yb_in)
-    relay("lateup", 4, 8, late_up, yc_out, yc_in)
+    relay("lateup", ((2, 6), (4, 8)), raw_up + late_up, yb_out, yb_in)
 
     inner = (lane >= 4) & (lane < nz - 4)
 
@@ -448,7 +467,6 @@
         for k in range(3):
             sw[k] = jnp.where(left, results[0][k], results[1][k])
 
-    relay("rawlow", 3, 6, raw_low, ye_out, ye_in)
     with scope("endswait"):
         arrived(1, 12 * ny // 8)
     with scope("strippack"):
@@ -472,11 +490,10 @@
             st[f, 1, 0:ny, :] = jnp.where(left, piece, corner[0])
             st[f, 2, 0:ny, :] = jnp.where(left, rot(zr[1, f // 4], 4 - 4 * (f % 4), 1), mid)
             st[f, 3, 0:ny, :] = jnp.where(left, corner[1], piece)
-        y_start(10, strip_tiles, yd_out, yd_in)
+        y_start(8, strip_tiles, yd_out, yd_in)
 
     with scope("yup"):
-        y_finish(6, raw_up, yb_in)
-        y_finish(8, late_up, yc_in)
+        y_finish(6, raw_up + late_up, yb_in)
     with scope("upper"):
         p = last + 1
         first_range(p, p + 1)
@@ -494,16 +511,15 @@
         rr[0, p + 1] = (m0 - m0p) + (upper_in[7] + (y_down(q2) - q2) + (z_down(q1) - q1))
         rr[1, p + 1] = (m0p + m0) * 0.5
 
-    relay("latelow", 5, 6, late_low, yf_out, yf_in)
+    relay("latelow", ((3, 6), (5, 6)), raw_low + late_low, yc_out, yc_in)
     with scope("ystrip"):
-        y_finish(10, strip_tiles, yd_in)
+        y_finish(8, strip_tiles, yd_in)
     with scope("strips"):
         strips()
     with scope("outup"):
         outputs(first + 3, last + 1, None)
     with scope("ylow"):
-        y_finish(7, raw_low, ye_in)
-        y_finish(9, late_low, yf_in)
+        y_finish(7, raw_low + late_low, yc_in)
     with scope("lower"):
         p = first - 1
         first_range(p, p + 1)
@@ -527,7 +543,7 @@
     hbm = pl.BlockSpec(memory_space=pl.ANY)
     sides = 1 if sizes[1] == 2 else 2
     relays = []
-    for count in (6 * nx, 6, 6, 24, 6, 6):
+    for count in (6 * nx, 12, 12, 24):
         relays += [pltpu.VMEM((count, 8, nz), f32), pltpu.VMEM((sides, count, 8, nz), f32)]
     return pl.pallas_call(
         functools.partial(kernel, sizes, nx, ny, nz),
@@ -560,7 +576,7 @@
             pltpu.VMEM((320, 8, nz), f32),
             pltpu.SemaphoreType.DMA((2,)),
             pltpu.SemaphoreType.DMA((1,)),
-            pltpu.SemaphoreType.DMA((11,)),
+            pltpu.SemaphoreType.DMA((9,)),
             pltpu.SemaphoreType.REGULAR((2,)),
         ],
         compiler_params=pltpu.CompilerParams(

time: 13.9 us -> 13.8 us (level)
  the two profiles are of different devices: /device:TPU:25 before, /device:TPU:5 now
where the time goes in v5:
time: 13.8 us; the launch traced here: 13.7 us
  Pallas kernels  13 us (94%)
  local copies, waits for them, and re-layouts  0.68 us (5%)
    pallas_call x1, Pallas kernels, on_device(): pl.pallas_call(functools.partial(kernel, sizes, nx, ny, nz), out_shape=pl...  13 us
    unnamed x1, local copies, waits for them, and re-layouts  0.68 us

profile of v5, /device:TPU:5, one launch (start us, length us, event | category | flops | bytes accessed | tf_op | source)
XLA Modules:
  0.0 13.7 jit_solution(6046591955601597471)
XLA Ops:
  0.0 13.0 %shard_map.55 = f32[3,8,16,128]{3,2,1,0:T(8,128)S(1)} custom-call(f32[8]{0:T(128)} %cond_hbm.1, f32[3,8,16,128]{3,2,1,0:T(8,128)} %rhs_hbm.1, f32[3,8,16,128]{3,2,1,0:T(8,128)} %frac_hbm.1, s32[8,16,128]{2,1,0:T(8,128)} %reg_hbm.1, s32[3,8,16,128]{3,2,1,0:T(8,128)} %flag_hbm.1), custom_call_target="tpu_custom_call" | custom-call | tf_op jit(solution)/shard_map/pallas_call | solution.py:548
  13.0 0.7 %copy.7 = f32[3,8,16,128]{3,2,1,0:T(8,128)} copy(f32[3,8,16,128]{3,2,1,0:T(8,128)S(1)} %shard_map.55) | data formatting | bytes 393216

commit v6 on v5

--- a/solution.py
+++ b/solution.py
@@ -56,16 +56,11 @@
 
 
 def jacobi_scale(ks):
-    return damping / jnp.where(ks > 0.0, 4.0 + ks, 1.0)
-
-
-def start_iter(rhs, ks):
-    return jnp.where(ks > 0.0, jacobi_scale(ks) * rhs, 0.0)
-
-
-def next_iter(rhs, ks, u, cc):
-    new = u + jacobi_scale(ks) * (rhs - (cc + ks * u))
-    return jnp.where(ks > 0.0, new, 0.0)
+    return jnp.where(ks > 0.0, damping / (4.0 + ks), 0.0)
+
+
+def next_iter(rhs, ks, scale, u, cc):
+    return u + scale * (rhs - (cc + ks * u))
 
 
 def masked_residual(rhs, ks, u, cc):
@@ -96,7 +91,7 @@
 def kernel(
     sizes, nx, ny, nz, cond_hbm, rhs_hbm, frac_hbm, reg_hbm, flag_hbm, out_ref,
     cond, frac_ref, reg_ref, flag_ref,
-    e, st, sw, u1, u2, mm, rr, zs, zr, ds, dr, ends_out, ends_in, lower_out, lower_in, upper_out, upper_in,
+    e, st, sw, jac, u1, u2, mm, rr, zs, zr, ds, dr, dx_out, dx_in, ends_out, ends_in, lower_out, lower_in, upper_out, upper_in,
     ya_out, ya_in, yb_out, yb_in, yc_out, yc_in, yd_out, yd_in,
     blank, load, send, recv, near,
 ):
@@ -126,6 +121,7 @@
         greet(*(on(0, gx=x, gz=z) for x, z in steps))
     else:
         greet(device(gx=1), device(gx=-1), device(gy=1), device(gy=-1), *(device(gx=x, gz=z) for x, z in steps))
+        greet(*(device(gx=x, gy=y, gz=z) for x, z in steps if x for y in (1, -1)))
     own_rows = pl.ds(0, ny)
     loads = [
         pltpu.make_async_copy(src, dst, load.at[i])
@@ -150,7 +146,7 @@
                 pl.semaphore_wait(barrier, 5)
                 pl.semaphore_signal(near.at[0], inc=1, device_id=device(gy=1), device_id_type=MESH)
         else:
-            pl.semaphore_wait(barrier, 4 + len(steps))
+            pl.semaphore_wait(barrier, 12 + len(steps))
 
         loads[4].wait()
         wait_tiles(load.at[0], 10 * nx * ny // 8)
@@ -222,7 +218,11 @@
             other = rot(tiles[1], half, 1)
             ds[0, side] = jnp.where(low_half, other, tiles[0])
             ds[1, side] = jnp.where(low_half, tiles[0], other)
-        starts = [start_iter(packs[k], packs[3 + k]) for k in range(3)]
+            if side == 1:
+                for i in range(2):
+                    tile = jnp.where(low_half == (i == 0), other, tiles[0])
+                    dx_out[i] = jnp.where(row < 4, tile[0:8], tile[ny - 8:ny])
+        starts = [jacobi_scale(packs[3 + k]) * packs[k] for k in range(3)]
         moves = (
             [(f, packs[f], 1, 2 * f, 2) for f in range(6)] + [(k, starts[k], 3, 11 + k, 1) for k in (1, 2)],
             [(f, packs[f], nx - 2, 2 * f, 2) for f in range(6)] + [(k, starts[k], nx - 3, 12 + k, 1) for k in range(3)],
@@ -264,13 +264,18 @@
         copy(3, e.at[:, last, own_rows], e.at[:, first - 1, own_rows], up, False),
     ]
     late_copies = [
-        copy(4, upper_out, upper_in.at[:, own_rows], down, False),
+        copy(4, upper_out.at[pl.ds(0, 6)], upper_in.at[pl.ds(0, 6)], down, False),
         copy(5, lower_out, lower_in.at[:, own_rows], up, False),
     ]
+    last_copy = copy(9, upper_out.at[pl.ds(6, 2), own_rows], upper_in.at[pl.ds(6, 2), own_rows], down, False)
     z_copies = [copy(1, zs.at[0], zr.at[0], device(gz=-1), False), copy(1, zs.at[1], zr.at[1], device(gz=1), False)]
     corner_copies = [
-        copy(1, ds.at[side, zside], dr.at[side, zside], device(gx=1 - 2 * side, gz=2 * zside - 1), False)
+        copy(1 + 9 * zside, ds.at[side, zside], dr.at[side, zside], device(gx=1 - 2 * side, gz=2 * zside - 1), False)
         for side in range(2) for zside in range(2)
+    ]
+    cross_copies = [
+        copy(10, dx_out.at[side], dx_in.at[i, side], device(gx=1 - 2 * side, gy=2 * i - 1, gz=1), False)
+        for side in range(2) for i in range(1 if paired else 2)
     ]
 
     def start(*copies):
@@ -282,18 +287,26 @@
 
     def start_both():
         start_far(1)
+        start(*cross_copies)
         start_far(0)
 
-    up_first = (lax.rem(pos["gx"], 4) == 3) & (pos["gz"] == 0)
+    down_first = (lax.rem(pos["gx"], 4) == 1) & (pos["gz"] == 0)
 
     def in_order(begin):
-        pl.when(up_first)(lambda: begin(1, 0))
-        pl.when(jnp.logical_not(up_first))(lambda: begin(0, 1))
+        pl.when(down_first)(lambda: begin(0, 1))
+        pl.when(jnp.logical_not(down_first))(lambda: begin(1, 0))
 
     late_start = pos["gz"] == 0
     in_order(lambda a, b: start(ends_copies[a], ends_copies[b]))
 
-    in_order(lambda a, b: start(raw_copies[a]))
+    up_only = lax.rem(pos["gx"], 4) == 3
+
+    def on_start():
+        pl.when(down_first)(lambda: start(raw_copies[0]))
+        pl.when(up_only)(lambda: start(raw_copies[1]))
+        pl.when(jnp.logical_not(down_first | up_only))(lambda: start(raw_copies[1], raw_copies[0]))
+
+    on_start()
 
     @pl.when(jnp.logical_not(late_start))
     def _():
@@ -317,7 +330,7 @@
             f1m, f2m = f1, f2
 
     def emit_second(k, p, cc):
-        u2[k, p] = next_iter(e[k, p], e[3 + k, p], u1[k, p], cc)
+        u2[k, p] = next_iter(e[k, p], e[3 + k, p], jac[k, p], u1[k, p], cc)
 
     def emit_masked(k, p, cc):
         mm[k, p] = masked_residual(e[k, p], e[3 + k, p], u2[k, p], cc)
@@ -335,7 +348,9 @@
     def first_range(lo, hi):
         for p in range(lo, hi):
             for k in range(3):
-                u1[k, p] = start_iter(e[k, p], e[3 + k, p])
+                scale = jacobi_scale(e[3 + k, p])
+                jac[k, p] = scale
+                u1[k, p] = scale * e[k, p]
 
     def below(v, p):
         up0 = v[0, p]
@@ -357,14 +372,18 @@
         mm[0, p] = m0
         sent = (u1[1, p], u1[2, p], e[4, p], e[5, p], u2[1, p], u2[2, p], m0, (y_down(m1) - m1) + (z_down(m2) - m2))
         for i, v in enumerate(sent):
-            upper_out[i] = v[0:ny]
-    @pl.when(up_first)
+            upper_out[i] = v
+    @pl.when(down_first)
     def _():
-        start(raw_copies[0], late_copies[1], late_copies[0])
-
-    @pl.when(jnp.logical_not(up_first))
+        start(late_copies[0], last_copy, raw_copies[1], late_copies[1])
+
+    @pl.when(up_only)
     def _():
-        start(late_copies[0], raw_copies[1], late_copies[1])
+        start(late_copies[1], raw_copies[0], late_copies[0], last_copy)
+
+    @pl.when(jnp.logical_not(down_first | up_only))
+    def _():
+        start(late_copies[1], late_copies[0], last_copy)
 
     with scope("inner2"):
         curl_sweep(u2, faces(u2, first + 1), first + 2, last - 1, emit_masked)
@@ -376,25 +395,24 @@
             far_wait()
             start_both()
 
-    def relay(name, groups, places, out, into):
+    def relay(name, groups, relayed, places, out, into):
         with scope(name):
             for group, count in groups:
                 arrived(group, count * ny // 8)
-            y_start(4 + groups[0][0], places, out, into)
+            y_start(relayed, places, out, into)
 
     raw_up = [(e, (f, last + 1)) for f in range(6)]
     raw_low = [(e, (f, first - 1)) for f in range(6)]
-    late_up = [(upper_in, (i,)) for i in range(6)]
     late_low = [(lower_in, (i,)) for i in range(6)]
     strip_tiles = [(st, (f, t)) for f in range(6) for t in range(4)]
-    relay("lateup", ((2, 6), (4, 8)), raw_up + late_up, yb_out, yb_in)
+    relay("rawup", ((2, 6),), 6, raw_up, yb_out, yb_in)
 
     inner = (lane >= 4) & (lane < nz - 4)
 
     def node_at(p, count=4):
         return [nodal_step(rr[q, p], rr[q, p - 1], rr[q, p + 1]) for q in range(count)]
 
-    def outputs(lo, hi, kept):
+    def outputs(lo, hi):
         s_next = node_at(lo)
         for p in range(lo, hi):
             s = s_next
@@ -413,62 +431,66 @@
     slot24 = lane24 // SEG
     left24 = (lane24 % SEG) < 8
 
+    span = range(4)
+
     def x_up(vs):
         rs = [rot(v, -SEG, 1) for v in vs]
-        return [jnp.where(lane24 < nz - SEG, rs[t], rs[(t + 1) % len(rs)]) for t in range(len(rs))]
+        return [jnp.where(lane24 < nz - SEG, rs[t], rs[t ^ 1]) for t in span]
 
     def x_down(vs):
         rs = [rot(v, SEG, 1) for v in vs]
-        return [jnp.where(lane24 >= SEG, rs[t], rs[t - 1]) for t in range(len(rs))]
-
-    span = range(2)
+        return [jnp.where(lane24 >= SEG, rs[t], rs[t ^ 1]) for t in span]
 
     def strip_curl(u):
         u1p, u2p = x_up(u[1]), x_up(u[2])
-        f0 = [face_zero(u[1][t], u[2][t]) for t in span]
         f1 = [face_one(u[0][t], u[2][t], u2p[t]) for t in span]
         f2 = [face_two(u[0][t], u[1][t], u1p[t]) for t in span]
+        f0 = [face_zero(u[1][t], u[2][t]) for t in span]
         f1m, f2m = x_down(f1), x_down(f2)
         out = [edges(f0[t], f1[t], f2[t], f1m[t], f2m[t]) for t in span]
         return [[out[t][k] for t in span] for k in range(3)]
 
     def strips():
+        sr = [[st[k, t] for t in span] for k in range(3)]
+        sk = [[st[3 + k, t] for t in span] for k in range(3)]
+        outer = (slot24 == 3) | (slot24 == nx - 3)
+        scale = [[jacobi_scale(sk[k][t]) for t in span] for k in range(3)]
+        u = [[scale[k][t] * sr[k][t] for t in span] for k in range(3)]
+        for k in range(3):
+            u[k][1] = jnp.where(outer & left24, sr[k][1], u[k][1])
+            u[k][3] = jnp.where(outer & ~left24, sr[k][3], u[k][3])
+        cc = strip_curl(u)
+        u = [[next_iter(sr[k][t], sk[k][t], scale[k][t], u[k][t], cc[k][t]) for t in span] for k in range(3)]
+        cc = strip_curl(u)
+        m = [[masked_residual(sr[k][t], sk[k][t], u[k][t], cc[k][t]) for t in span] for k in range(3)]
+        m0m = x_down(m[0])
+        r = [nodal_rhs(m[0][t], m0m[t], m[1][t], m[2][t]) for t in span]
+        s = []
+        for q in range(4):
+            rq = [r[t][q] for t in span]
+            rm, rp = x_down(rq), x_up(rq)
+            s.append([nodal_step(rq[t], rm[t], rp[t]) if q < 2 or t % 2 == 0 else None for t in span])
+        s0p, s1p = x_up(s[0]), x_up(s[1])
         results = []
-        for base in (0, 2):
-            def sr(k, t):
-                return st[k, base + t]
-
-            def sk(k, t):
-                return st[3 + k, base + t]
-
-            sent = ((slot24 == 3) | (slot24 == nx - 3)) & (left24 if base == 0 else ~left24)
-            u = [[start_iter(sr(k, t), sk(k, t)) for t in span] for k in range(3)]
-            for k in range(3):
-                u[k][1] = jnp.where(sent, sr(k, 1), u[k][1])
-            cc = strip_curl(u)
-            u = [[next_iter(sr(k, t), sk(k, t), u[k][t], cc[k][t]) for t in span] for k in range(3)]
-            cc = strip_curl(u)
-            m = [[masked_residual(sr(k, t), sk(k, t), u[k][t], cc[k][t]) for t in span] for k in range(3)]
-            m0m = x_down(m[0])
-            r = [nodal_rhs(m[0][t], m0m[t], m[1][t], m[2][t]) for t in span]
-            s = []
-            for q in range(4):
-                rq = [r[t][q] for t in span]
-                rm, rp = x_down(rq), x_up(rq)
-                s.append([nodal_step(rq[t], rm[t], rp[t]) for t in span])
-            s0p, s1p = x_up(s[0])[0], x_up(s[1])[0]
-            s0, s1, s2, s3 = [s[q][0] for q in range(4)]
+        for t in (0, 2):
+            s0, s1, s2, s3 = [s[q][t] for q in range(4)]
             corr = (
-                (s0p - s0) + (s1 + s1p) * 0.5,
+                (s0p[t] - s0) + (s1 + s1p[t]) * 0.5,
                 (y_up(s0) - s0) + (s2 + y_up(s2)) * 0.5,
                 (z_up(s0) - s0) + (s3 + z_up(s3)) * 0.5,
             )
-            results.append([finish(sr(k, 0), sk(k, 0), u[k][0], corr[k])[0:ny] for k in range(3)])
+            results.append([finish(sr[k][t], sk[k][t], u[k][t], corr[k])[0:ny] for k in range(3)])
         for k in range(3):
             sw[k] = jnp.where(left, results[0][k], results[1][k])
 
+    def corner_of(f, plus, minus, off):
+        low = low_half[0:plus.shape[0]]
+        if f < 4:
+            return rot(jnp.where(low, plus, minus), off - 4 * f, 1)
+        return rot(jnp.where(low, minus, plus), half + off - 4 * (f - 4), 1)
+
     with scope("endswait"):
-        arrived(1, 12 * ny // 8)
+        arrived(1, 10 * ny // 8)
     with scope("strippack"):
         for f in range(6):
             t, to = divmod(2 * f, 8)
@@ -478,59 +500,60 @@
             if f < 3:
                 piece = jnp.where(slot == 3, rot(ends_in[0, 1], SEG * (3 - (3 + f)), 1), piece)
                 piece = jnp.where(slot == nx - 3, rot(ends_in[1, 1], SEG * (nx - 3 - (4 + f)), 1), piece)
-            corner = []
-            for zside, off in ((0, 8), (1, 4)):
-                plus, minus = dr[1, zside], dr[0, zside]
-                if f < 4:
-                    corner.append(rot(jnp.where(low_half, plus, minus), off - 4 * f, 1))
-                else:
-                    corner.append(rot(jnp.where(low_half, minus, plus), half + off - 4 * (f - 4), 1))
             mid = packs[f]
             st[f, 0, 0:ny, :] = jnp.where(left, mid, rot(zr[0, f // 4], 8 - 4 * (f % 4), 1))
-            st[f, 1, 0:ny, :] = jnp.where(left, piece, corner[0])
+            st[f, 1, 0:ny, :] = jnp.where(left, piece, corner_of(f, dr[1, 0], dr[0, 0], 8))
             st[f, 2, 0:ny, :] = jnp.where(left, rot(zr[1, f // 4], 4 - 4 * (f % 4), 1), mid)
-            st[f, 3, 0:ny, :] = jnp.where(left, corner[1], piece)
+            st[f, 3, 0:ny, :] = piece
         y_start(8, strip_tiles, yd_out, yd_in)
 
-    with scope("yup"):
-        y_finish(6, raw_up + late_up, yb_in)
-    with scope("upper"):
-        p = last + 1
-        first_range(p, p + 1)
-        f1 = face_one(u1[0, p], u1[2, p], upper_in[1])
-        f2 = face_two(u1[0, p], u1[1, p], upper_in[0])
-        curl_sweep(u1, faces(u1, last - 1), last, p + 1, emit_second, (f1, f2))
-        f1 = face_one(u2[0, p], u2[2, p], upper_in[5])
-        f2 = face_two(u2[0, p], u2[1, p], upper_in[4])
-        curl_sweep(u2, faces(u2, last - 2), last - 1, p + 1, emit_masked, (f1, f2))
-        node_range(last - 1, p + 1)
-        v0 = u2[0, p]
-        q2 = jnp.where(upper_in[2] > 0.0, u2[1, p] + (y_up(v0) - v0), 0.0)
-        q1 = jnp.where(upper_in[3] > 0.0, (z_up(v0) - v0) + u2[2, p], 0.0)
-        m0, m0p = mm[0, p], upper_in[6]
-        rr[0, p + 1] = (m0 - m0p) + (upper_in[7] + (y_down(q2) - q2) + (z_down(q1) - q1))
-        rr[1, p + 1] = (m0p + m0) * 0.5
-
-    relay("latelow", ((3, 6), (5, 6)), raw_low + late_low, yc_out, yc_in)
-    with scope("ystrip"):
-        y_finish(8, strip_tiles, yd_in)
-    with scope("strips"):
-        strips()
-    with scope("outup"):
-        outputs(first + 3, last + 1, None)
-    with scope("ylow"):
-        y_finish(7, raw_low + late_low, yc_in)
-    with scope("lower"):
-        p = first - 1
-        first_range(p, p + 1)
-        curl_sweep(u1, (lower_in[0] - u1[2, p], u1[1, p] - lower_in[1]), p, first + 1, emit_second)
-        f1, f2 = lower_in[3] - u2[2, p], u2[1, p] - lower_in[4]
-        cc = (z_down(f1) - f1) - (y_down(f2) - f2)
-        mm[0, p - 1] = jnp.where(lower_in[2] > 0.0, lower_in[5] - cc, 0.0)
-        curl_sweep(u2, (f1, f2), p, first + 2, emit_rest)
-        node_range(p, first + 2)
-    with scope("outlow"):
-        outputs(first, first + 3, None)
+    relay("latelow", ((3, 6), (5, 6)), 7, raw_low + late_low, yc_out, yc_in)
+    def side_strips():
+        with scope("ystrip"):
+            y_finish(8, strip_tiles, yd_in)
+            arrived(10, 2 * (ny // 8 + dx_in.shape[0]))
+            cross = [dx_in[0, i] if paired else jnp.where(row < 4, dx_in[0, i], dx_in[1, i]) for i in range(2)]
+            for f in range(6):
+                st[f, 3, 0:ny, :] = jnp.where(left, corner_of(f, dr[1, 1], dr[0, 1], 4), st[f, 3, 0:ny, :])
+                st[f, 3, ny:ny + 8, :] = jnp.where(left[0:8], corner_of(f, cross[1], cross[0], 4), st[f, 3, ny:ny + 8, :])
+        with scope("strips"):
+            strips()
+
+    def both_sides():
+        with scope("ylow"):
+            y_finish(7, raw_low + late_low, yc_in)
+        with scope("yup"):
+            y_finish(6, raw_up, yb_in)
+            arrived(4, 6 * (ny + 8) // 8)
+            arrived(9, 2 * ny // 8)
+        with scope("sides"):
+            p = first - 1
+            first_range(p, p + 1)
+            curl_sweep(u1, (lower_in[0] - u1[2, p], u1[1, p] - lower_in[1]), p, first + 1, emit_second)
+            f1, f2 = lower_in[3] - u2[2, p], u2[1, p] - lower_in[4]
+            cc = (z_down(f1) - f1) - (y_down(f2) - f2)
+            mm[0, p - 1] = jnp.where(lower_in[2] > 0.0, lower_in[5] - cc, 0.0)
+            curl_sweep(u2, (f1, f2), p, first + 2, emit_rest)
+            node_range(p, first + 2)
+            p = last + 1
+            first_range(p, p + 1)
+            f1 = face_one(u1[0, p], u1[2, p], upper_in[1])
+            f2 = face_two(u1[0, p], u1[1, p], upper_in[0])
+            curl_sweep(u1, faces(u1, last - 1), last, p + 1, emit_second, (f1, f2))
+            f1 = face_one(u2[0, p], u2[2, p], upper_in[5])
+            f2 = face_two(u2[0, p], u2[1, p], upper_in[4])
+            curl_sweep(u2, faces(u2, last - 2), last - 1, p + 1, emit_masked, (f1, f2))
+            node_range(last - 1, p + 1)
+            v0 = u2[0, p]
+            q2 = jnp.where(upper_in[2] > 0.0, u2[1, p] + (y_up(v0) - v0), 0.0)
+            q1 = jnp.where(upper_in[3] > 0.0, (z_up(v0) - v0) + u2[2, p], 0.0)
+            m0, m0p = mm[0, p], upper_in[6]
+            rr[0, p + 1] = (m0 - m0p) + (upper_in[7] + (y_down(q2) - q2) + (z_down(q1) - q1))
+            rr[1, p + 1] = (m0p + m0) * 0.5
+            outputs(first, last + 1)
+
+    side_strips()
+    both_sides()
     with scope("sendwait"):
         wait_tiles(send.at[0], sum(sent_tiles))
 
@@ -543,7 +566,7 @@
     hbm = pl.BlockSpec(memory_space=pl.ANY)
     sides = 1 if sizes[1] == 2 else 2
     relays = []
-    for count in (6 * nx, 12, 12, 24):
+    for count in (6 * nx, 6, 12, 24):
         relays += [pltpu.VMEM((count, 8, nz), f32), pltpu.VMEM((sides, count, 8, nz), f32)]
     return pl.pallas_call(
         functools.partial(kernel, sizes, nx, ny, nz),
@@ -561,22 +584,25 @@
             pltpu.VMEM((3, planes, rows, nz), f32),
             pltpu.VMEM((3, planes, rows, nz), f32),
             pltpu.VMEM((3, planes, rows, nz), f32),
+            pltpu.VMEM((3, planes, rows, nz), f32),
             pltpu.VMEM((4, planes, rows, nz), f32),
             pltpu.VMEM((2, 2, ny, nz), f32),
             pltpu.VMEM((2, 2, ny, nz), f32),
             pltpu.VMEM((2, 2, ny, nz), f32),
             pltpu.VMEM((2, 2, ny, nz), f32),
+            pltpu.VMEM((2, 8, nz), f32),
+            pltpu.VMEM((sides, 2, 8, nz), f32),
             pltpu.VMEM((2, 2, ny, nz), f32),
             pltpu.VMEM((2, 2, ny, nz), f32),
             pltpu.VMEM((6, ny, nz), f32),
             pltpu.VMEM((6, rows, nz), f32),
-            pltpu.VMEM((8, ny, nz), f32),
+            pltpu.VMEM((8, rows, nz), f32),
             pltpu.VMEM((8, rows, nz), f32),
             *relays,
             pltpu.VMEM((320, 8, nz), f32),
             pltpu.SemaphoreType.DMA((2,)),
             pltpu.SemaphoreType.DMA((1,)),
-            pltpu.SemaphoreType.DMA((9,)),
+            pltpu.SemaphoreType.DMA((11,)),
             pltpu.SemaphoreType.REGULAR((2,)),
         ],
         compiler_params=pltpu.CompilerParams(

time: 13.8 us -> 13.8 us (level)
  no operation moved by 1% of the time
where the time goes in v6:
time: 13.8 us; the launch traced here: 13.7 us
  Pallas kernels  13 us (94%)
  local copies, waits for them, and re-layouts  0.68 us (5%)
    pallas_call x1, Pallas kernels, on_device(): pl.pallas_call(functools.partial(kernel, sizes, nx, ny, nz), out_shape=pl...  13 us
    unnamed x1, local copies, waits for them, and re-layouts  0.68 us

profile of v6, /device:TPU:5, one launch (start us, length us, event | category | flops | bytes accessed | tf_op | source)
XLA Modules:
  0.0 13.7 jit_solution(115951107756828007)
XLA Ops:
  0.0 13.0 %shard_map.55 = f32[3,8,16,128]{3,2,1,0:T(8,128)S(1)} custom-call(f32[8]{0:T(128)} %cond_hbm.1, f32[3,8,16,128]{3,2,1,0:T(8,128)} %rhs_hbm.1, f32[3,8,16,128]{3,2,1,0:T(8,128)} %frac_hbm.1, s32[8,16,128]{2,1,0:T(8,128)} %reg_hbm.1, s32[3,8,16,128]{3,2,1,0:T(8,128)} %flag_hbm.1), custom_call_target="tpu_custom_call" | custom-call | tf_op jit(solution)/shard_map/pallas_call | solution.py:571
  13.0 0.7 %copy.7 = f32[3,8,16,128]{3,2,1,0:T(8,128)} copy(f32[3,8,16,128]{3,2,1,0:T(8,128)S(1)} %shard_map.55) | data formatting | bytes 393216

commit v7 on v6

--- a/solution.py
+++ b/solution.py
@@ -91,8 +91,8 @@
 def kernel(
     sizes, nx, ny, nz, cond_hbm, rhs_hbm, frac_hbm, reg_hbm, flag_hbm, out_ref,
     cond, frac_ref, reg_ref, flag_ref,
-    e, st, sw, jac, u1, u2, mm, rr, zs, zr, ds, dr, dx_out, dx_in, ends_out, ends_in, lower_out, lower_in, upper_out, upper_in,
-    ya_out, ya_in, yb_out, yb_in, yc_out, yc_in, yd_out, yd_in,
+    e, st, sw, jac, u1, u2, mm, rr, zs, zr, ds, dr, dx_out, dx_in, zx_out, zx_in, ends_out, ends_in, lower_out, lower_in, upper_out, upper_in,
+    ya_out, ya_in, yb_out, yb_in, yc_out, yc_in, yd_out, yd_in, ye_out, ye_in,
     blank, load, send, recv, near,
 ):
     gx, gy, gz = sizes
@@ -121,7 +121,7 @@
         greet(*(on(0, gx=x, gz=z) for x, z in steps))
     else:
         greet(device(gx=1), device(gx=-1), device(gy=1), device(gy=-1), *(device(gx=x, gz=z) for x, z in steps))
-        greet(*(device(gx=x, gy=y, gz=z) for x, z in steps if x for y in (1, -1)))
+        greet(*(device(gx=x, gy=y, gz=z) for x, z in steps for y in (1, -1)))
     own_rows = pl.ds(0, ny)
     loads = [
         pltpu.make_async_copy(src, dst, load.at[i])
@@ -146,7 +146,7 @@
                 pl.semaphore_wait(barrier, 5)
                 pl.semaphore_signal(near.at[0], inc=1, device_id=device(gy=1), device_id_type=MESH)
         else:
-            pl.semaphore_wait(barrier, 12 + len(steps))
+            pl.semaphore_wait(barrier, 4 + 3 * len(steps))
 
         loads[4].wait()
         wait_tiles(load.at[0], 10 * nx * ny // 8)
@@ -215,6 +215,7 @@
                 tiles[f // 4] = pick(tiles[f // 4], quad == f % 4, rot(packs[f], 4 * (f % 4) - off, 1))
             for i in range(2):
                 zs[side, i] = tiles[i]
+                zx_out[side, i] = jnp.where(row < 4, tiles[i][0:8], tiles[i][ny - 8:ny])
             other = rot(tiles[1], half, 1)
             ds[0, side] = jnp.where(low_half, other, tiles[0])
             ds[1, side] = jnp.where(low_half, tiles[0], other)
@@ -265,10 +266,14 @@
     ]
     late_copies = [
         copy(4, upper_out.at[pl.ds(0, 6)], upper_in.at[pl.ds(0, 6)], down, False),
-        copy(5, lower_out, lower_in.at[:, own_rows], up, False),
+        copy(5, lower_out.at[:, own_rows], lower_in.at[:, own_rows], up, False),
     ]
+    wide_copy = pltpu.make_async_remote_copy(
+        src_ref=lower_out, dst_ref=lower_in, send_sem=send.at[0], recv_sem=recv.at[5],
+        device_id=up, device_id_type=MESH,
+    )
     last_copy = copy(9, upper_out.at[pl.ds(6, 2), own_rows], upper_in.at[pl.ds(6, 2), own_rows], down, False)
-    z_copies = [copy(1, zs.at[0], zr.at[0], device(gz=-1), False), copy(1, zs.at[1], zr.at[1], device(gz=1), False)]
+    z_copies = [copy(10, zs.at[i], zr.at[i], device(gz=2 * i - 1), False) for i in range(2)]
     corner_copies = [
         copy(1 + 9 * zside, ds.at[side, zside], dr.at[side, zside], device(gx=1 - 2 * side, gz=2 * zside - 1), False)
         for side in range(2) for zside in range(2)
@@ -276,6 +281,9 @@
     cross_copies = [
         copy(10, dx_out.at[side], dx_in.at[i, side], device(gx=1 - 2 * side, gy=2 * i - 1, gz=1), False)
         for side in range(2) for i in range(1 if paired else 2)
+    ] + [
+        copy(10, zx_out.at[side], zx_in.at[i, side], device(gy=2 * i - 1, gz=2 * side - 1), False)
+        for side in range(2) for i in range(1 if paired else 2)
     ]
 
     def start(*copies):
@@ -291,6 +299,8 @@
         start_far(0)
 
     down_first = (lax.rem(pos["gx"], 4) == 1) & (pos["gz"] == 0)
+    wide = (lax.rem(device(gx=-1)["gx"], 4) == 1) & (pos["gz"] == 0)
+    narrow = jnp.logical_not(wide)
 
     def in_order(begin):
         pl.when(down_first)(lambda: begin(0, 1))
@@ -364,7 +374,7 @@
         p = last - 1
         sent = (*below(u1, p), e[3, p], *below(u2, p), e[0, p] - e[3, p] * u2[0, p])
         for i, v in enumerate(sent):
-            lower_out[i] = v[0:ny]
+            lower_out[i] = v
         p = first + 1
         f1, f2 = faces(u2, p)
         cc = edges(face_zero(u2[1, p], u2[2, p]), f1, f2, -u2[2, p], u2[1, p])
@@ -375,7 +385,7 @@
             upper_out[i] = v
     @pl.when(down_first)
     def _():
-        start(late_copies[0], last_copy, raw_copies[1], late_copies[1])
+        start(late_copies[0], last_copy, raw_copies[1], wide_copy)
 
     @pl.when(up_only)
     def _():
@@ -490,7 +500,7 @@
         return rot(jnp.where(low, minus, plus), half + off - 4 * (f - 4), 1)
 
     with scope("endswait"):
-        arrived(1, 10 * ny // 8)
+        arrived(1, 6 * ny // 8)
     with scope("strippack"):
         for f in range(6):
             t, to = divmod(2 * f, 8)
@@ -501,27 +511,47 @@
                 piece = jnp.where(slot == 3, rot(ends_in[0, 1], SEG * (3 - (3 + f)), 1), piece)
                 piece = jnp.where(slot == nx - 3, rot(ends_in[1, 1], SEG * (nx - 3 - (4 + f)), 1), piece)
             mid = packs[f]
-            st[f, 0, 0:ny, :] = jnp.where(left, mid, rot(zr[0, f // 4], 8 - 4 * (f % 4), 1))
+            st[f, 0, 0:ny, :] = mid
             st[f, 1, 0:ny, :] = jnp.where(left, piece, corner_of(f, dr[1, 0], dr[0, 0], 8))
-            st[f, 2, 0:ny, :] = jnp.where(left, rot(zr[1, f // 4], 4 - 4 * (f % 4), 1), mid)
+            st[f, 2, 0:ny, :] = mid
             st[f, 3, 0:ny, :] = piece
         y_start(8, strip_tiles, yd_out, yd_in)
 
-    relay("latelow", ((3, 6), (5, 6)), 7, raw_low + late_low, yc_out, yc_in)
+    relay("rawlow", ((3, 6),), 7, raw_low, yc_out, yc_in)
+
+    @pl.when(narrow)
+    def _():
+        relay("latelow", ((5, 6),), 11, late_low, ye_out, ye_in)
+
     def side_strips():
         with scope("ystrip"):
             y_finish(8, strip_tiles, yd_in)
-            arrived(10, 2 * (ny // 8 + dx_in.shape[0]))
-            cross = [dx_in[0, i] if paired else jnp.where(row < 4, dx_in[0, i], dx_in[1, i]) for i in range(2)]
+            sides = dx_in.shape[0]
+            arrived(10, 6 * (ny // 8 + sides))
+
+            def crossed(ref, *where):
+                if paired:
+                    return ref[(0, *where)]
+                return jnp.where(row < 4, ref[(0, *where)], ref[(1, *where)])
+
             for f in range(6):
-                st[f, 3, 0:ny, :] = jnp.where(left, corner_of(f, dr[1, 1], dr[0, 1], 4), st[f, 3, 0:ny, :])
-                st[f, 3, ny:ny + 8, :] = jnp.where(left[0:8], corner_of(f, cross[1], cross[0], 4), st[f, 3, ny:ny + 8, :])
+                t, q = divmod(f, 4)
+                for rows, above, below_z, plus, minus in (
+                    (slice(0, ny), zr[0, t], zr[1, t], dr[1, 1], dr[0, 1]),
+                    (halo, crossed(zx_in, 0, t), crossed(zx_in, 1, t), crossed(dx_in, 1), crossed(dx_in, 0)),
+                ):
+                    mine = left[0:above.shape[0]]
+                    st[f, 0, rows, :] = jnp.where(mine, st[f, 0, rows, :], rot(above, 8 - 4 * q, 1))
+                    st[f, 2, rows, :] = jnp.where(mine, rot(below_z, 4 - 4 * q, 1), st[f, 2, rows, :])
+                    st[f, 3, rows, :] = jnp.where(mine, corner_of(f, plus, minus, 4), st[f, 3, rows, :])
         with scope("strips"):
             strips()
 
     def both_sides():
         with scope("ylow"):
-            y_finish(7, raw_low + late_low, yc_in)
+            y_finish(7, raw_low, yc_in)
+            pl.when(narrow)(lambda: y_finish(11, late_low, ye_in))
+            pl.when(wide)(lambda: arrived(5, 6 * (ny + 8) // 8))
         with scope("yup"):
             y_finish(6, raw_up, yb_in)
             arrived(4, 6 * (ny + 8) // 8)
@@ -555,7 +585,10 @@
     side_strips()
     both_sides()
     with scope("sendwait"):
-        wait_tiles(send.at[0], sum(sent_tiles))
+        total = sum(sent_tiles)
+        pl.when(down_first)(lambda: wait_tiles(send.at[0], total + 6))
+        pl.when(wide)(lambda: wait_tiles(send.at[0], total - 6 * dx_in.shape[0]))
+        pl.when(jnp.logical_not(down_first | wide))(lambda: wait_tiles(send.at[0], total))
 
 
 def on_device(sizes, rhs, conductivity, fraction, region, flags):
@@ -566,7 +599,7 @@
     hbm = pl.BlockSpec(memory_space=pl.ANY)
     sides = 1 if sizes[1] == 2 else 2
     relays = []
-    for count in (6 * nx, 6, 12, 24):
+    for count in (6 * nx, 6, 6, 24, 6):
         relays += [pltpu.VMEM((count, 8, nz), f32), pltpu.VMEM((sides, count, 8, nz), f32)]
     return pl.pallas_call(
         functools.partial(kernel, sizes, nx, ny, nz),
@@ -592,9 +625,11 @@
             pltpu.VMEM((2, 2, ny, nz), f32),
             pltpu.VMEM((2, 8, nz), f32),
             pltpu.VMEM((sides, 2, 8, nz), f32),
+            pltpu.VMEM((2, 2, 8, nz), f32),
+            pltpu.VMEM((sides, 2, 2, 8, nz), f32),
             pltpu.VMEM((2, 2, ny, nz), f32),
             pltpu.VMEM((2, 2, ny, nz), f32),
-            pltpu.VMEM((6, ny, nz), f32),
+            pltpu.VMEM((6, rows, nz), f32),
             pltpu.VMEM((6, rows, nz), f32),
             pltpu.VMEM((8, rows, nz), f32),
             pltpu.VMEM((8, rows, nz), f32),
@@ -602,7 +637,7 @@
             pltpu.VMEM((320, 8, nz), f32),
             pltpu.SemaphoreType.DMA((2,)),
             pltpu.SemaphoreType.DMA((1,)),
-            pltpu.SemaphoreType.DMA((11,)),
+            pltpu.SemaphoreType.DMA((12,)),
             pltpu.SemaphoreType.REGULAR((2,)),
         ],
         compiler_params=pltpu.CompilerParams(

time: 13.8 us -> 13 us (0.942)
  Pallas kernels: 13 us -> 12.2 us
    pallas_call x1, Pallas kernels: 13 us -> 12.2 us  [on_device(): pl.pallas_call(functools.partial(kernel, sizes, nx, ny, nz), out_shape=pl...]
where the time goes in v7:
time: 13 us; the launch traced here: 12.9 us
  Pallas kernels  12.2 us (94%)
  local copies, waits for them, and re-layouts  0.68 us (5%)
    pallas_call x1, Pallas kernels, on_device(): pl.pallas_call(functools.partial(kernel, sizes, nx, ny, nz), out_shape=pl...  12.2 us
    unnamed x1, local copies, waits for them, and re-layouts  0.68 us

profile of v7, /device:TPU:5, one launch (start us, length us, event | category | flops | bytes accessed | tf_op | source)
XLA Modules:
  0.0 12.9 jit_solution(7057669501020333362)
XLA Ops:
  0.0 12.2 %shard_map.55 = f32[3,8,16,128]{3,2,1,0:T(8,128)S(1)} custom-call(f32[8]{0:T(128)} %cond_hbm.1, f32[3,8,16,128]{3,2,1,0:T(8,128)} %rhs_hbm.1, f32[3,8,16,128]{3,2,1,0:T(8,128)} %frac_hbm.1, s32[8,16,128]{2,1,0:T(8,128)} %reg_hbm.1, s32[3,8,16,128]{3,2,1,0:T(8,128)} %flag_hbm.1), custom_call_target="tpu_custom_call" | custom-call | tf_op jit(solution)/shard_map/pallas_call | solution.py:604
  12.2 0.7 %copy.7 = f32[3,8,16,128]{3,2,1,0:T(8,128)} copy(f32[3,8,16,128]{3,2,1,0:T(8,128)S(1)} %shard_map.55) | data formatting | bytes 393216

commit v8 on v7

--- a/solution.py
+++ b/solution.py
@@ -92,7 +92,7 @@
     sizes, nx, ny, nz, cond_hbm, rhs_hbm, frac_hbm, reg_hbm, flag_hbm, out_ref,
     cond, frac_ref, reg_ref, flag_ref,
     e, st, sw, jac, u1, u2, mm, rr, zs, zr, ds, dr, dx_out, dx_in, zx_out, zx_in, ends_out, ends_in, lower_out, lower_in, upper_out, upper_in,
-    ya_out, ya_in, yb_out, yb_in, yc_out, yc_in, yd_out, yd_in, ye_out, ye_in,
+    ya_out, ya_in, yb_out, yb_in, yc_out, yc_in, yd_out, yd_in, ye_out, ye_in, yf_out, yf_in,
     blank, load, send, recv, near,
 ):
     gx, gy, gz = sizes
@@ -140,14 +140,6 @@
     with scope("load"):
         for one in loads:
             one.start()
-        if paired:
-            @pl.when(pos["gy"] == 1)
-            def _():
-                pl.semaphore_wait(barrier, 5)
-                pl.semaphore_signal(near.at[0], inc=1, device_id=device(gy=1), device_id_type=MESH)
-        else:
-            pl.semaphore_wait(barrier, 4 + 3 * len(steps))
-
         loads[4].wait()
         wait_tiles(load.at[0], 10 * nx * ny // 8)
 
@@ -219,28 +211,34 @@
             other = rot(tiles[1], half, 1)
             ds[0, side] = jnp.where(low_half, other, tiles[0])
             ds[1, side] = jnp.where(low_half, tiles[0], other)
-            if side == 1:
-                for i in range(2):
-                    tile = jnp.where(low_half == (i == 0), other, tiles[0])
-                    dx_out[i] = jnp.where(row < 4, tile[0:8], tile[ny - 8:ny])
+            for i in range(2):
+                tile = jnp.where(low_half == (i == 0), other, tiles[0])
+                dx_out[i, side] = jnp.where(row < 4, tile[0:8], tile[ny - 8:ny])
         starts = [jacobi_scale(packs[3 + k]) * packs[k] for k in range(3)]
         moves = (
-            [(f, packs[f], 1, 2 * f, 2) for f in range(6)] + [(k, starts[k], 3, 11 + k, 1) for k in (1, 2)],
-            [(f, packs[f], nx - 2, 2 * f, 2) for f in range(6)] + [(k, starts[k], nx - 3, 12 + k, 1) for k in range(3)],
+            [(packs[f], 0, 8 * (f // 2) + 3 * (f % 2), 3) for f in range(6)] + [(starts[k], 3, 5 + k, 1) for k in (1, 2)],
+            [(packs[f], nx - 2, 2 * f, 2) for f in range(6)] + [(starts[k], nx - 3, 12 + k, 1) for k in range(3)],
         )
         for side in range(2):
-            tiles = [None, None]
-            for f, v, at, to, wide in moves[side]:
+            tiles = [None, None, None]
+            for v, at, to, wide in moves[side]:
                 t, to = divmod(to, 8)
                 tiles[t] = pick(tiles[t], (slot >= to) & (slot < to + wide), rot(v, SEG * (to - at), 1))
-            for i in range(2):
-                ends_out[side, i] = tiles[i]
+            for i in range(3 - side):
+                ends_out[3 * side + i] = tiles[i]
 
     with scope("barrierwait"):
         if paired:
+            @pl.when(pos["gy"] == 1)
+            def _():
+                pl.semaphore_wait(barrier, 5)
+                pl.semaphore_signal(near.at[0], inc=1, device_id=device(gy=1), device_id_type=MESH)
+
             @pl.when(pos["gy"] == 0)
             def _():
                 pl.semaphore_wait(near.at[0], 1)
+        else:
+            pl.semaphore_wait(barrier, 4 + 3 * len(steps))
 
     def far_wait():
         if not paired:
@@ -259,31 +257,47 @@
     y_start(0, own, ya_out, ya_in)
 
     up, down = device(gx=1), device(gx=-1)
-    ends_copies = [copy(1, ends_out.at[0], ends_in.at[0], down, False), copy(1, ends_out.at[1], ends_in.at[1], up, False)]
+    ends_copies = [copy(12, ends_out.at[pl.ds(0, 3)], ends_in.at[pl.ds(0, 3)], down, False), copy(12, ends_out.at[pl.ds(3, 2)], ends_in.at[pl.ds(3, 2)], up, False)]
     raw_copies = [
         copy(2, e.at[:, first, own_rows], e.at[:, last + 1, own_rows], down, False),
         copy(3, e.at[:, last, own_rows], e.at[:, first - 1, own_rows], up, False),
     ]
     late_copies = [
-        copy(4, upper_out.at[pl.ds(0, 6)], upper_in.at[pl.ds(0, 6)], down, False),
+        copy(4, upper_out.at[pl.ds(0, 4)], upper_in.at[pl.ds(0, 4)], down, False),
         copy(5, lower_out.at[:, own_rows], lower_in.at[:, own_rows], up, False),
     ]
     wide_copy = pltpu.make_async_remote_copy(
         src_ref=lower_out, dst_ref=lower_in, send_sem=send.at[0], recv_sem=recv.at[5],
         device_id=up, device_id_type=MESH,
     )
-    last_copy = copy(9, upper_out.at[pl.ds(6, 2), own_rows], upper_in.at[pl.ds(6, 2), own_rows], down, False)
-    z_copies = [copy(10, zs.at[i], zr.at[i], device(gz=2 * i - 1), False) for i in range(2)]
+    thin_copies = [
+        pltpu.make_async_remote_copy(
+            src_ref=src, dst_ref=dst, send_sem=send.at[0], recv_sem=recv.at[4], device_id=down, device_id_type=MESH
+        )
+        for src, dst in (
+            (upper_out.at[pl.ds(0, 4), own_rows], upper_in.at[pl.ds(0, 4), own_rows]),
+            (e.at[4, first + 1, own_rows], e.at[4, last + 2, own_rows]),
+        )
+    ]
+    last_copy = copy(9, upper_out.at[pl.ds(4, 2), own_rows], upper_in.at[pl.ds(4, 2), own_rows], down, False)
+    mask_copies = [
+        copy(4, e.at[4, first + 1], e.at[4, last + 2], down, False),
+        copy(4, e.at[5, first + 1, own_rows], e.at[5, last + 2, own_rows], down, False),
+    ]
+    z_copies = [copy(10 - 9 * i, zs.at[i], zr.at[i], device(gz=2 * i - 1), False) for i in range(2)]
     corner_copies = [
-        copy(1 + 9 * zside, ds.at[side, zside], dr.at[side, zside], device(gx=1 - 2 * side, gz=2 * zside - 1), False)
+        copy(10 - 9 * zside, ds.at[side, zside], dr.at[side, zside], device(gx=1 - 2 * side, gz=2 * zside - 1), False)
         for side in range(2) for zside in range(2)
     ]
     cross_copies = [
-        copy(10, dx_out.at[side], dx_in.at[i, side], device(gx=1 - 2 * side, gy=2 * i - 1, gz=1), False)
-        for side in range(2) for i in range(1 if paired else 2)
-    ] + [
-        copy(10, zx_out.at[side], zx_in.at[i, side], device(gy=2 * i - 1, gz=2 * side - 1), False)
-        for side in range(2) for i in range(1 if paired else 2)
+        [
+            copy(10 - 9 * zside, dx_out.at[side, zside], dx_in.at[i, side, zside], device(gx=1 - 2 * side, gy=2 * i - 1, gz=2 * zside - 1), False)
+            for side in range(2) for i in range(1 if paired else 2)
+        ] + [
+            copy(10 - 9 * zside, zx_out.at[zside], zx_in.at[i, zside], device(gy=2 * i - 1, gz=2 * zside - 1), False)
+            for i in range(1 if paired else 2)
+        ]
+        for zside in range(2)
     ]
 
     def start(*copies):
@@ -294,13 +308,14 @@
         start(corner_copies[zside], corner_copies[2 + zside], z_copies[zside])
 
     def start_both():
-        start_far(1)
-        start(*cross_copies)
-        start_far(0)
+        for zside in (1, 0):
+            start_far(zside)
+            start(*cross_copies[zside])
 
     down_first = (lax.rem(pos["gx"], 4) == 1) & (pos["gz"] == 0)
     wide = (lax.rem(device(gx=-1)["gx"], 4) == 1) & (pos["gz"] == 0)
     narrow = jnp.logical_not(wide)
+    thin = (lax.rem(device(gx=1)["gx"], 4) == 1) & (pos["gz"] == 0)
 
     def in_order(begin):
         pl.when(down_first)(lambda: begin(0, 1))
@@ -310,13 +325,8 @@
     in_order(lambda a, b: start(ends_copies[a], ends_copies[b]))
 
     up_only = lax.rem(pos["gx"], 4) == 3
-
-    def on_start():
-        pl.when(down_first)(lambda: start(raw_copies[0]))
-        pl.when(up_only)(lambda: start(raw_copies[1]))
-        pl.when(jnp.logical_not(down_first | up_only))(lambda: start(raw_copies[1], raw_copies[0]))
-
-    on_start()
+    pl.when(jnp.logical_not(up_only))(lambda: start(raw_copies[0]))
+    pl.when(jnp.logical_not(down_first))(lambda: start(raw_copies[1]))
 
     @pl.when(jnp.logical_not(late_start))
     def _():
@@ -380,20 +390,20 @@
         cc = edges(face_zero(u2[1, p], u2[2, p]), f1, f2, -u2[2, p], u2[1, p])
         m0, m1, m2 = [masked_residual(e[k, p], e[3 + k, p], u2[k, p], cc[k]) for k in range(3)]
         mm[0, p] = m0
-        sent = (u1[1, p], u1[2, p], e[4, p], e[5, p], u2[1, p], u2[2, p], m0, (y_down(m1) - m1) + (z_down(m2) - m2))
+        sent = (u1[1, p], u1[2, p], u2[1, p], u2[2, p], m0, (y_down(m1) - m1) + (z_down(m2) - m2))
         for i, v in enumerate(sent):
             upper_out[i] = v
     @pl.when(down_first)
     def _():
-        start(late_copies[0], last_copy, raw_copies[1], wide_copy)
+        start(mask_copies[1], *thin_copies, last_copy, raw_copies[1], wide_copy)
 
     @pl.when(up_only)
     def _():
-        start(late_copies[1], raw_copies[0], late_copies[0], last_copy)
+        start(late_copies[1], raw_copies[0], *mask_copies, late_copies[0], last_copy)
 
     @pl.when(jnp.logical_not(down_first | up_only))
     def _():
-        start(late_copies[1], late_copies[0], last_copy)
+        start(late_copies[1], *mask_copies, late_copies[0], last_copy)
 
     with scope("inner2"):
         curl_sweep(u2, faces(u2, first + 1), first + 2, last - 1, emit_masked)
@@ -415,7 +425,6 @@
     raw_low = [(e, (f, first - 1)) for f in range(6)]
     late_low = [(lower_in, (i,)) for i in range(6)]
     strip_tiles = [(st, (f, t)) for f in range(6) for t in range(4)]
-    relay("rawup", ((2, 6),), 6, raw_up, yb_out, yb_in)
 
     inner = (lane >= 4) & (lane < nz - 4)
 
@@ -441,7 +450,7 @@
     slot24 = lane24 // SEG
     left24 = (lane24 % SEG) < 8
 
-    span = range(4)
+    span = range(2)
 
     def x_up(vs):
         rs = [rot(v, -SEG, 1) for v in vs]
@@ -460,15 +469,14 @@
         out = [edges(f0[t], f1[t], f2[t], f1m[t], f2m[t]) for t in span]
         return [[out[t][k] for t in span] for k in range(3)]
 
-    def strips():
-        sr = [[st[k, t] for t in span] for k in range(3)]
-        sk = [[st[3 + k, t] for t in span] for k in range(3)]
+    def strips(base):
+        sr = [[st[k, 2 * base + t] for t in span] for k in range(3)]
+        sk = [[st[3 + k, 2 * base + t] for t in span] for k in range(3)]
         outer = (slot24 == 3) | (slot24 == nx - 3)
         scale = [[jacobi_scale(sk[k][t]) for t in span] for k in range(3)]
         u = [[scale[k][t] * sr[k][t] for t in span] for k in range(3)]
         for k in range(3):
-            u[k][1] = jnp.where(outer & left24, sr[k][1], u[k][1])
-            u[k][3] = jnp.where(outer & ~left24, sr[k][3], u[k][3])
+            u[k][1] = jnp.where(outer & (left24 if base == 0 else ~left24), sr[k][1], u[k][1])
         cc = strip_curl(u)
         u = [[next_iter(sr[k][t], sk[k][t], scale[k][t], u[k][t], cc[k][t]) for t in span] for k in range(3)]
         cc = strip_curl(u)
@@ -481,17 +489,15 @@
             rm, rp = x_down(rq), x_up(rq)
             s.append([nodal_step(rq[t], rm[t], rp[t]) if q < 2 or t % 2 == 0 else None for t in span])
         s0p, s1p = x_up(s[0]), x_up(s[1])
-        results = []
-        for t in (0, 2):
-            s0, s1, s2, s3 = [s[q][t] for q in range(4)]
-            corr = (
-                (s0p[t] - s0) + (s1 + s1p[t]) * 0.5,
-                (y_up(s0) - s0) + (s2 + y_up(s2)) * 0.5,
-                (z_up(s0) - s0) + (s3 + z_up(s3)) * 0.5,
-            )
-            results.append([finish(sr[k][t], sk[k][t], u[k][t], corr[k])[0:ny] for k in range(3)])
+        s0, s1, s2, s3 = [s[q][0] for q in range(4)]
+        corr = (
+            (s0p[0] - s0) + (s1 + s1p[0]) * 0.5,
+            (y_up(s0) - s0) + (s2 + y_up(s2)) * 0.5,
+            (z_up(s0) - s0) + (s3 + z_up(s3)) * 0.5,
+        )
         for k in range(3):
-            sw[k] = jnp.where(left, results[0][k], results[1][k])
+            result = finish(sr[k][0], sk[k][0], u[k][0], corr[k])[0:ny]
+            sw[k] = result if base == 0 else jnp.where(left, sw[k], result)
 
     def corner_of(f, plus, minus, off):
         low = low_half[0:plus.shape[0]]
@@ -500,63 +506,61 @@
         return rot(jnp.where(low, minus, plus), half + off - 4 * (f - 4), 1)
 
     with scope("endswait"):
-        arrived(1, 6 * ny // 8)
+        arrived(12, 5 * ny // 8)
     with scope("strippack"):
         for f in range(6):
             t, to = divmod(2 * f, 8)
-            piece = rot(ends_in[0, t], SEG * (1 - to), 1)
-            piece = jnp.where(slot == 0, end_piece(e[f, last + 1, 0:ny, :], 0), piece)
-            piece = jnp.where(slot >= nx - 2, rot(ends_in[1, t], SEG * (nx - 2 - to), 1), piece)
+            piece = rot(ends_in[f // 2], SEG * (0 - 3 * (f % 2)), 1)
+            piece = jnp.where(slot >= nx - 2, rot(ends_in[3 + t], SEG * (nx - 2 - to), 1), piece)
             if f < 3:
-                piece = jnp.where(slot == 3, rot(ends_in[0, 1], SEG * (3 - (3 + f)), 1), piece)
-                piece = jnp.where(slot == nx - 3, rot(ends_in[1, 1], SEG * (nx - 3 - (4 + f)), 1), piece)
+                piece = jnp.where(slot == 3, rot(ends_in[0], SEG * (3 - (5 + f)), 1), piece)
+                piece = jnp.where(slot == nx - 3, rot(ends_in[4], SEG * (nx - 3 - (4 + f)), 1), piece)
             mid = packs[f]
             st[f, 0, 0:ny, :] = mid
-            st[f, 1, 0:ny, :] = jnp.where(left, piece, corner_of(f, dr[1, 0], dr[0, 0], 8))
+            st[f, 1, 0:ny, :] = piece
             st[f, 2, 0:ny, :] = mid
             st[f, 3, 0:ny, :] = piece
         y_start(8, strip_tiles, yd_out, yd_in)
 
-    relay("rawlow", ((3, 6),), 7, raw_low, yc_out, yc_in)
-
-    @pl.when(narrow)
-    def _():
-        relay("latelow", ((5, 6),), 11, late_low, ye_out, ye_in)
-
-    def side_strips():
+
+    def crossed(ref, *where):
+        if paired:
+            return ref[(0, *where)]
+        return jnp.where(row < 4, ref[(0, *where)], ref[(1, *where)])
+
+    def strip_inputs(base):
         with scope("ystrip"):
-            y_finish(8, strip_tiles, yd_in)
-            sides = dx_in.shape[0]
-            arrived(10, 6 * (ny // 8 + sides))
-
-            def crossed(ref, *where):
-                if paired:
-                    return ref[(0, *where)]
-                return jnp.where(row < 4, ref[(0, *where)], ref[(1, *where)])
-
+            if base == 0:
+                y_finish(8, strip_tiles, yd_in)
+            arrived(10 - 9 * base, 4 * (ny // 8 + dx_in.shape[0]))
+            off = 8 - 4 * base
             for f in range(6):
                 t, q = divmod(f, 4)
-                for rows, above, below_z, plus, minus in (
-                    (slice(0, ny), zr[0, t], zr[1, t], dr[1, 1], dr[0, 1]),
-                    (halo, crossed(zx_in, 0, t), crossed(zx_in, 1, t), crossed(dx_in, 1), crossed(dx_in, 0)),
+                for rows, tile, corners in (
+                    (slice(0, ny), zr[base, t], [dr[i, base] for i in range(2)]),
+                    (halo, crossed(zx_in, base, t), [crossed(dx_in, i, base) for i in range(2)]),
                 ):
-                    mine = left[0:above.shape[0]]
-                    st[f, 0, rows, :] = jnp.where(mine, st[f, 0, rows, :], rot(above, 8 - 4 * q, 1))
-                    st[f, 2, rows, :] = jnp.where(mine, rot(below_z, 4 - 4 * q, 1), st[f, 2, rows, :])
-                    st[f, 3, rows, :] = jnp.where(mine, corner_of(f, plus, minus, 4), st[f, 3, rows, :])
-        with scope("strips"):
-            strips()
-
-    def both_sides():
+                    mine = left[0:tile.shape[0]] if base == 0 else ~left[0:tile.shape[0]]
+                    for at, piece in ((2 * base, rot(tile, off - 4 * q, 1)), (2 * base + 1, corner_of(f, corners[1], corners[0], off))):
+                        st[f, at, rows, :] = jnp.where(mine, st[f, at, rows, :], piece)
+
+    late_up = [(upper_in, (i,)) for i in range(4)] + [(e, (4, last + 2))]
+
+    def lower_inputs():
         with scope("ylow"):
             y_finish(7, raw_low, yc_in)
             pl.when(narrow)(lambda: y_finish(11, late_low, ye_in))
             pl.when(wide)(lambda: arrived(5, 6 * (ny + 8) // 8))
+
+    def upper_inputs():
         with scope("yup"):
             y_finish(6, raw_up, yb_in)
-            arrived(4, 6 * (ny + 8) // 8)
+            pl.when(jnp.logical_not(thin))(lambda: arrived(4, (5 * (ny + 8) + ny) // 8))
+            pl.when(thin)(lambda: y_finish(0, late_up, yf_in))
             arrived(9, 2 * ny // 8)
-        with scope("sides"):
+
+    def lower_side():
+        with scope("lower"):
             p = first - 1
             first_range(p, p + 1)
             curl_sweep(u1, (lower_in[0] - u1[2, p], u1[1, p] - lower_in[1]), p, first + 1, emit_second)
@@ -565,30 +569,59 @@
             mm[0, p - 1] = jnp.where(lower_in[2] > 0.0, lower_in[5] - cc, 0.0)
             curl_sweep(u2, (f1, f2), p, first + 2, emit_rest)
             node_range(p, first + 2)
+
+    def upper_side():
+        with scope("upper"):
             p = last + 1
             first_range(p, p + 1)
             f1 = face_one(u1[0, p], u1[2, p], upper_in[1])
             f2 = face_two(u1[0, p], u1[1, p], upper_in[0])
             curl_sweep(u1, faces(u1, last - 1), last, p + 1, emit_second, (f1, f2))
-            f1 = face_one(u2[0, p], u2[2, p], upper_in[5])
-            f2 = face_two(u2[0, p], u2[1, p], upper_in[4])
+            f1 = face_one(u2[0, p], u2[2, p], upper_in[3])
+            f2 = face_two(u2[0, p], u2[1, p], upper_in[2])
             curl_sweep(u2, faces(u2, last - 2), last - 1, p + 1, emit_masked, (f1, f2))
             node_range(last - 1, p + 1)
             v0 = u2[0, p]
-            q2 = jnp.where(upper_in[2] > 0.0, u2[1, p] + (y_up(v0) - v0), 0.0)
-            q1 = jnp.where(upper_in[3] > 0.0, (z_up(v0) - v0) + u2[2, p], 0.0)
-            m0, m0p = mm[0, p], upper_in[6]
-            rr[0, p + 1] = (m0 - m0p) + (upper_in[7] + (y_down(q2) - q2) + (z_down(q1) - q1))
+            q2 = jnp.where(e[4, p + 1] > 0.0, u2[1, p] + (y_up(v0) - v0), 0.0)
+            q1 = jnp.where(e[5, p + 1] > 0.0, (z_up(v0) - v0) + u2[2, p], 0.0)
+            m0, m0p = mm[0, p], upper_in[4]
+            rr[0, p + 1] = (m0 - m0p) + (upper_in[5] + (y_down(q2) - q2) + (z_down(q1) - q1))
             rr[1, p + 1] = (m0p + m0) * 0.5
+
+    def in_turn(*pieces):
+        for piece in pieces:
+            piece()
+
+    def write_all():
+        with scope("out"):
             outputs(first, last + 1)
 
-    side_strips()
-    both_sides()
+    def side_strips(base):
+        strip_inputs(base)
+        with scope("strips"):
+            strips(base)
+
+    side_strips(0)
+    relay("rawup", ((2, 6),), 6, raw_up, yb_out, yb_in)
+    relay("rawlow", ((3, 6),), 7, raw_low, yc_out, yc_in)
+
+    @pl.when(narrow)
+    def _():
+        relay("latelow", ((5, 6),), 11, late_low, ye_out, ye_in)
+
+    @pl.when(thin)
+    def _():
+        relay("lateup", ((4, 6),), 0, late_up, yf_out, yf_in)
+
+    side_strips(1)
+    in_turn(lower_inputs, upper_inputs, lower_side, upper_side, write_all)
     with scope("sendwait"):
-        total = sum(sent_tiles)
-        pl.when(down_first)(lambda: wait_tiles(send.at[0], total + 6))
-        pl.when(wide)(lambda: wait_tiles(send.at[0], total - 6 * dx_in.shape[0]))
-        pl.when(jnp.logical_not(down_first | wide))(lambda: wait_tiles(send.at[0], total))
+        sides = dx_in.shape[0]
+        total = sum(sent_tiles) - 5 * sides
+        pl.when(down_first)(lambda: wait_tiles(send.at[0], total + 1))
+        pl.when(wide)(lambda: wait_tiles(send.at[0], total - 6 * sides))
+        pl.when(thin)(lambda: wait_tiles(send.at[0], total + 5 * sides))
+        pl.when(jnp.logical_not(down_first | wide | thin))(lambda: wait_tiles(send.at[0], total))
 
 
 def on_device(sizes, rhs, conductivity, fraction, region, flags):
@@ -599,7 +632,7 @@
     hbm = pl.BlockSpec(memory_space=pl.ANY)
     sides = 1 if sizes[1] == 2 else 2
     relays = []
-    for count in (6 * nx, 6, 6, 24, 6):
+    for count in (6 * nx, 6, 6, 24, 6, 5):
         relays += [pltpu.VMEM((count, 8, nz), f32), pltpu.VMEM((sides, count, 8, nz), f32)]
     return pl.pallas_call(
         functools.partial(kernel, sizes, nx, ny, nz),
@@ -623,21 +656,21 @@
             pltpu.VMEM((2, 2, ny, nz), f32),
             pltpu.VMEM((2, 2, ny, nz), f32),
             pltpu.VMEM((2, 2, ny, nz), f32),
-            pltpu.VMEM((2, 8, nz), f32),
-            pltpu.VMEM((sides, 2, 8, nz), f32),
             pltpu.VMEM((2, 2, 8, nz), f32),
             pltpu.VMEM((sides, 2, 2, 8, nz), f32),
-            pltpu.VMEM((2, 2, ny, nz), f32),
-            pltpu.VMEM((2, 2, ny, nz), f32),
+            pltpu.VMEM((2, 2, 8, nz), f32),
+            pltpu.VMEM((sides, 2, 2, 8, nz), f32),
+            pltpu.VMEM((5, ny, nz), f32),
+            pltpu.VMEM((5, ny, nz), f32),
             pltpu.VMEM((6, rows, nz), f32),
             pltpu.VMEM((6, rows, nz), f32),
-            pltpu.VMEM((8, rows, nz), f32),
-            pltpu.VMEM((8, rows, nz), f32),
+            pltpu.VMEM((6, rows, nz), f32),
+            pltpu.VMEM((6, rows, nz), f32),
             *relays,
             pltpu.VMEM((320, 8, nz), f32),
             pltpu.SemaphoreType.DMA((2,)),
             pltpu.SemaphoreType.DMA((1,)),
-            pltpu.SemaphoreType.DMA((12,)),
+            pltpu.SemaphoreType.DMA((13,)),
             pltpu.SemaphoreType.REGULAR((2,)),
         ],
         compiler_params=pltpu.CompilerParams(

time: 13 us -> 12.8 us (0.985)
  the two profiles are of different devices: /device:TPU:5 before, /device:TPU:0 now
where the time goes in v8:
time: 12.8 us; the launch traced here: 12.6 us
  Pallas kernels  12 us (94%)
  local copies, waits for them, and re-layouts  0.68 us (5%)
    pallas_call x1, Pallas kernels, on_device(): pl.pallas_call(functools.partial(kernel, sizes, nx, ny, nz), out_shape=pl...  12 us
    unnamed x1, local copies, waits for them, and re-layouts  0.68 us

profile of v8, /device:TPU:0, one launch (start us, length us, event | category | flops | bytes accessed | tf_op | source)
XLA Modules:
  0.0 12.6 jit_solution(9974663157971404817)
XLA Ops:
  0.0 12.0 %shard_map.55 = f32[3,8,16,128]{3,2,1,0:T(8,128)S(1)} custom-call(f32[8]{0:T(128)} %cond_hbm.1, f32[3,8,16,128]{3,2,1,0:T(8,128)} %rhs_hbm.1, f32[3,8,16,128]{3,2,1,0:T(8,128)} %frac_hbm.1, s32[8,16,128]{2,1,0:T(8,128)} %reg_hbm.1, s32[3,8,16,128]{3,2,1,0:T(8,128)} %flag_hbm.1), custom_call_target="tpu_custom_call" | custom-call | tf_op jit(solution)/shard_map/pallas_call | solution.py:637
  12.0 0.7 %copy.7 = f32[3,8,16,128]{3,2,1,0:T(8,128)} copy(f32[3,8,16,128]{3,2,1,0:T(8,128)S(1)} %shard_map.55) | data formatting | bytes 393216

commit v9 on v8

--- a/solution.py
+++ b/solution.py
@@ -548,13 +548,11 @@
 
     def lower_inputs():
         with scope("ylow"):
-            y_finish(7, raw_low, yc_in)
             pl.when(narrow)(lambda: y_finish(11, late_low, ye_in))
             pl.when(wide)(lambda: arrived(5, 6 * (ny + 8) // 8))
 
     def upper_inputs():
         with scope("yup"):
-            y_finish(6, raw_up, yb_in)
             pl.when(jnp.logical_not(thin))(lambda: arrived(4, (5 * (ny + 8) + ny) // 8))
             pl.when(thin)(lambda: y_finish(0, late_up, yf_in))
             arrived(9, 2 * ny // 8)
@@ -562,25 +560,23 @@
     def lower_side():
         with scope("lower"):
             p = first - 1
-            first_range(p, p + 1)
-            curl_sweep(u1, (lower_in[0] - u1[2, p], u1[1, p] - lower_in[1]), p, first + 1, emit_second)
+            curl_sweep(u1, (lower_in[0] - u1[2, p], u1[1, p] - lower_in[1]), p, first, emit_second)
             f1, f2 = lower_in[3] - u2[2, p], u2[1, p] - lower_in[4]
             cc = (z_down(f1) - f1) - (y_down(f2) - f2)
             mm[0, p - 1] = jnp.where(lower_in[2] > 0.0, lower_in[5] - cc, 0.0)
-            curl_sweep(u2, (f1, f2), p, first + 2, emit_rest)
+            curl_sweep(u2, (f1, f2), p, first + 1, emit_masked)
             node_range(p, first + 2)
 
     def upper_side():
         with scope("upper"):
             p = last + 1
-            first_range(p, p + 1)
             f1 = face_one(u1[0, p], u1[2, p], upper_in[1])
             f2 = face_two(u1[0, p], u1[1, p], upper_in[0])
-            curl_sweep(u1, faces(u1, last - 1), last, p + 1, emit_second, (f1, f2))
+            curl_sweep(u1, faces(u1, last), p, p + 1, emit_second, (f1, f2))
             f1 = face_one(u2[0, p], u2[2, p], upper_in[3])
             f2 = face_two(u2[0, p], u2[1, p], upper_in[2])
-            curl_sweep(u2, faces(u2, last - 2), last - 1, p + 1, emit_masked, (f1, f2))
-            node_range(last - 1, p + 1)
+            curl_sweep(u2, faces(u2, last - 1), last, p + 1, emit_masked, (f1, f2))
+            node_range(last, p + 1)
             v0 = u2[0, p]
             q2 = jnp.where(e[4, p + 1] > 0.0, u2[1, p] + (y_up(v0) - v0), 0.0)
             q1 = jnp.where(e[5, p + 1] > 0.0, (z_up(v0) - v0) + u2[2, p], 0.0)
@@ -601,23 +597,47 @@
         with scope("strips"):
             strips(base)
 
+    def raw_relays():
+        del sent_tiles[counted:]
+        relay("rawup", ((2, 6),), 6, raw_up, yb_out, yb_in)
+        relay("rawlow", ((3, 6),), 7, raw_low, yc_out, yc_in)
+
+    counted = len(sent_tiles)
+    strips_first = lax.rem(device(gx=1)["gx"], 4) == 3
+    pl.when(jnp.logical_not(strips_first))(lambda: raw_relays())
     side_strips(0)
-    relay("rawup", ((2, 6),), 6, raw_up, yb_out, yb_in)
-    relay("rawlow", ((3, 6),), 7, raw_low, yc_out, yc_in)
+    pl.when(strips_first)(lambda: raw_relays())
 
     @pl.when(narrow)
     def _():
         relay("latelow", ((5, 6),), 11, late_low, ye_out, ye_in)
 
+    base_tiles = sum(sent_tiles)
+
     @pl.when(thin)
     def _():
         relay("lateup", ((4, 6),), 0, late_up, yf_out, yf_in)
 
+    def raw_sides():
+        with scope("yraw"):
+            y_finish(7, raw_low, yc_in)
+            y_finish(6, raw_up, yb_in)
+        with scope("rawsides"):
+            first_range(first - 1, first)
+            first_range(last + 1, last + 2)
+            curl_sweep(u1, faces(u1, first - 1), first, first + 1, emit_second)
+            curl_sweep(u1, faces(u1, last - 1), last, last + 1, emit_second)
+            curl_sweep(u2, faces(u2, first), first + 1, first + 2, emit_rest)
+            curl_sweep(u2, faces(u2, last - 2), last - 1, last, emit_masked)
+            node_range(last - 1, last)
+
+    pl.when(thin)(raw_sides)
     side_strips(1)
+    pl.when(jnp.logical_not(thin))(raw_sides)
     in_turn(lower_inputs, upper_inputs, lower_side, upper_side, write_all)
     with scope("sendwait"):
+        total = base_tiles
         sides = dx_in.shape[0]
-        total = sum(sent_tiles) - 5 * sides
         pl.when(down_first)(lambda: wait_tiles(send.at[0], total + 1))
         pl.when(wide)(lambda: wait_tiles(send.at[0], total - 6 * sides))
         pl.when(thin)(lambda: wait_tiles(send.at[0], total + 5 * sides))

time: 12.8 us -> 12.7 us (level)
  no operation moved by 1% of the time
where the time goes in v9:
time: 12.7 us; the launch traced here: 12.6 us
  Pallas kernels  11.9 us (94%)
  local copies, waits for them, and re-layouts  0.68 us (5%)
    pallas_call x1, Pallas kernels, on_device(): pl.pallas_call(functools.partial(kernel, sizes, nx, ny, nz), out_shape=pl...  11.9 us
    unnamed x1, local copies, waits for them, and re-layouts  0.68 us

profile of v9, /device:TPU:0, one launch (start us, length us, event | category | flops | bytes accessed | tf_op | source)
XLA Modules:
  0.0 12.6 jit_solution(14781041929105345992)
XLA Ops:
  0.0 11.9 %shard_map.55 = f32[3,8,16,128]{3,2,1,0:T(8,128)S(1)} custom-call(f32[8]{0:T(128)} %cond_hbm.1, f32[3,8,16,128]{3,2,1,0:T(8,128)} %rhs_hbm.1, f32[3,8,16,128]{3,2,1,0:T(8,128)} %frac_hbm.1, s32[8,16,128]{2,1,0:T(8,128)} %reg_hbm.1, s32[3,8,16,128]{3,2,1,0:T(8,128)} %flag_hbm.1), custom_call_target="tpu_custom_call" | custom-call | tf_op jit(solution)/shard_map/pallas_call | solution.py:657
  11.9 0.7 %copy.7 = f32[3,8,16,128]{3,2,1,0:T(8,128)} copy(f32[3,8,16,128]{3,2,1,0:T(8,128)S(1)} %shard_map.55) | data formatting | bytes 393216

commit v10 on v9

--- a/solution.py
+++ b/solution.py
@@ -117,7 +117,7 @@
 
     if paired:
         greet(on(1, gx=1), on(1, gx=-1))
-        pl.when(pos["gy"] == 0)(lambda: greet(device(gy=1)))
+        greet(device(gy=1))
         greet(*(on(0, gx=x, gz=z) for x, z in steps))
     else:
         greet(device(gx=1), device(gx=-1), device(gy=1), device(gy=-1), *(device(gx=x, gz=z) for x, z in steps))
@@ -126,8 +126,10 @@
     loads = [
         pltpu.make_async_copy(src, dst, load.at[i])
         for src, dst, i in (
-            (rhs_hbm, e.at[pl.ds(0, 3), pl.ds(first, nx), own_rows], 0), (reg_hbm, reg_ref, 0),
-            (frac_hbm, frac_ref, 0), (flag_hbm, flag_ref, 0), (cond_hbm, cond, 1),
+            (cond_hbm, cond, 1), (reg_hbm, reg_ref, 0),
+            *((flag_hbm.at[k], flag_ref.at[k], 0) for k in range(3)),
+            *((frac_hbm.at[k], frac_ref.at[k], 0) for k in range(3)),
+            *((rhs_hbm.at[k], e.at[k, pl.ds(first, nx), own_rows], 0) for k in range(3)),
         )
     ]
 
@@ -140,8 +142,17 @@
     with scope("load"):
         for one in loads:
             one.start()
-        loads[4].wait()
+        loads[0].wait()
         wait_tiles(load.at[0], 10 * nx * ny // 8)
+
+    hurry = (lax.rem(pos["gx"], 4) == 3) & (pos["gz"] == gz - 1)
+
+    def far_collect():
+        pl.semaphore_wait(barrier, 1 + 2 * len(steps))
+        pl.semaphore_signal(near.at[1], inc=1, device_id=device(gy=1), device_id_type=MESH)
+
+    if paired:
+        pl.when((pos["gy"] == 0) & hurry)(lambda: far_collect())
 
     sent_tiles = []
 
@@ -181,6 +192,8 @@
     half = nz // 2
     low_half = lane < half
     quad = (lane % SEG) // 4
+    unit = (lane % SEG) // 3
+    spare = ((0, 3, 0), (1, 3, 3), (2, 3, 4), (nx - 2, 4, 0), (nx - 1, 4, 1))
     left = (lane % SEG) < 8
 
     def end_piece(v, j):
@@ -188,6 +201,34 @@
 
     def pick(base, where, other):
         return other if base is None else jnp.where(where, other, base)
+
+    z_copies = [copy(10 - 9 * i, zs.at[i], zr.at[i], device(gz=2 * i - 1), False) for i in range(2)]
+    corner_copies = [
+        copy(10 - 9 * zside, ds.at[side, zside], dr.at[side, zside], device(gx=1 - 2 * side, gz=2 * zside - 1), False)
+        for side in range(2) for zside in range(2)
+    ]
+    cross_copies = [
+        [
+            copy(10 - 9 * zside, dx_out.at[zside], dx_in.at[i, side, zside], device(gx=1 - 2 * side, gy=2 * i - 1, gz=2 * zside - 1), False)
+            for side in range(2) for i in range(1 if paired else 2)
+        ] + [
+            copy(10 - 9 * zside, zx_out.at[zside], zx_in.at[i, zside], device(gy=2 * i - 1, gz=2 * zside - 1), False)
+            for i in range(1 if paired else 2)
+        ]
+        for zside in range(2)
+    ]
+
+    def start(*copies):
+        for one in copies:
+            one.start()
+
+    def start_far(zside):
+        start(corner_copies[zside], corner_copies[2 + zside], z_copies[zside])
+
+    def start_both():
+        for zside in (1, 0):
+            start_far(zside)
+            start(*cross_copies[zside])
 
     packs = [None] * 6
     with scope("pack"):
@@ -201,6 +242,7 @@
                 e[3 + k, first + x, 0:ny, :] = ks
                 for f, v in ((k, e[k, first + x, 0:ny, :]), (3 + k, ks)):
                     packs[f] = pick(packs[f], slot == x, end_piece(v, x))
+        starts = [jacobi_scale(packs[3 + k]) * packs[k] for k in range(3)]
         for side, off in ((0, 8), (1, 4)):
             tiles = [None, None]
             for f in range(6):
@@ -208,13 +250,25 @@
             for i in range(2):
                 zs[side, i] = tiles[i]
                 zx_out[side, i] = jnp.where(row < 4, tiles[i][0:8], tiles[i][ny - 8:ny])
-            other = rot(tiles[1], half, 1)
-            ds[0, side] = jnp.where(low_half, other, tiles[0])
-            ds[1, side] = jnp.where(low_half, tiles[0], other)
-            for i in range(2):
-                tile = jnp.where(low_half == (i == 0), other, tiles[0])
-                dx_out[i, side] = jnp.where(row < 4, tile[0:8], tile[ny - 8:ny])
-        starts = [jacobi_scale(packs[3 + k]) * packs[k] for k in range(3)]
+            off = 8 - 3 * side
+            tile = None
+            for f in range(5):
+                tile = pick(tile, unit == f, rot(packs[f], 3 * f - off, 1))
+            for k in range(3):
+                outer = (slot == nx - 3) if k == 0 else (slot == 3) | (slot == nx - 3)
+                tile = pick(tile, outer & (unit == k), rot(starts[k], 3 * k - off, 1))
+            for at, to, u in spare:
+                tile = pick(tile, (slot == to) & (unit == u), rot(packs[5], SEG * (to - at) + 3 * u - off, 1))
+            upper, lower = tile[0:ny // 2], tile[ny // 2:ny]
+            ds[0, side] = jnp.where(low_half[0:ny // 2], rot(upper, half, 1), lower)
+            ds[1, side] = jnp.where(low_half[0:ny // 2], upper, rot(lower, half, 1))
+            dx_out[side] = jnp.where(row < 4, tile[0:8], tile[ny - 8:ny])
+        if paired:
+            @pl.when(hurry)
+            def _():
+                pl.when(pos["gy"] == 1)(lambda: pl.semaphore_wait(near.at[1], 1))
+                start_both()
+
         moves = (
             [(packs[f], 0, 8 * (f // 2) + 3 * (f % 2), 3) for f in range(6)] + [(starts[k], 3, 5 + k, 1) for k in (1, 2)],
             [(packs[f], nx - 2, 2 * f, 2) for f in range(6)] + [(starts[k], nx - 3, 12 + k, 1) for k in range(3)],
@@ -243,11 +297,7 @@
     def far_wait():
         if not paired:
             return
-
-        @pl.when(pos["gy"] == 0)
-        def _():
-            pl.semaphore_wait(barrier, 2 * len(steps))
-            pl.semaphore_signal(near.at[1], inc=1, device_id=device(gy=1), device_id_type=MESH)
+        pl.when(pos["gy"] == 0)(lambda: far_collect())
 
         @pl.when(pos["gy"] == 1)
         def _():
@@ -284,34 +334,6 @@
         copy(4, e.at[4, first + 1], e.at[4, last + 2], down, False),
         copy(4, e.at[5, first + 1, own_rows], e.at[5, last + 2, own_rows], down, False),
     ]
-    z_copies = [copy(10 - 9 * i, zs.at[i], zr.at[i], device(gz=2 * i - 1), False) for i in range(2)]
-    corner_copies = [
-        copy(10 - 9 * zside, ds.at[side, zside], dr.at[side, zside], device(gx=1 - 2 * side, gz=2 * zside - 1), False)
-        for side in range(2) for zside in range(2)
-    ]
-    cross_copies = [
-        [
-            copy(10 - 9 * zside, dx_out.at[side, zside], dx_in.at[i, side, zside], device(gx=1 - 2 * side, gy=2 * i - 1, gz=2 * zside - 1), False)
-            for side in range(2) for i in range(1 if paired else 2)
-        ] + [
-            copy(10 - 9 * zside, zx_out.at[zside], zx_in.at[i, zside], device(gy=2 * i - 1, gz=2 * zside - 1), False)
-            for i in range(1 if paired else 2)
-        ]
-        for zside in range(2)
-    ]
-
-    def start(*copies):
-        for one in copies:
-            one.start()
-
-    def start_far(zside):
-        start(corner_copies[zside], corner_copies[2 + zside], z_copies[zside])
-
-    def start_both():
-        for zside in (1, 0):
-            start_far(zside)
-            start(*cross_copies[zside])
-
     down_first = (lax.rem(pos["gx"], 4) == 1) & (pos["gz"] == 0)
     wide = (lax.rem(device(gx=-1)["gx"], 4) == 1) & (pos["gz"] == 0)
     narrow = jnp.logical_not(wide)
@@ -328,7 +350,7 @@
     pl.when(jnp.logical_not(up_only))(lambda: start(raw_copies[0]))
     pl.when(jnp.logical_not(down_first))(lambda: start(raw_copies[1]))
 
-    @pl.when(jnp.logical_not(late_start))
+    @pl.when(jnp.logical_not(late_start | (hurry if paired else late_start)))
     def _():
         with scope("nearwait"):
             far_wait()
@@ -476,7 +498,7 @@
         scale = [[jacobi_scale(sk[k][t]) for t in span] for k in range(3)]
         u = [[scale[k][t] * sr[k][t] for t in span] for k in range(3)]
         for k in range(3):
-            u[k][1] = jnp.where(outer & (left24 if base == 0 else ~left24), sr[k][1], u[k][1])
+            u[k][1] = jnp.where(outer, sr[k][1], u[k][1])
         cc = strip_curl(u)
         u = [[next_iter(sr[k][t], sk[k][t], scale[k][t], u[k][t], cc[k][t]) for t in span] for k in range(3)]
         cc = strip_curl(u)
@@ -499,11 +521,13 @@
             result = finish(sr[k][0], sk[k][0], u[k][0], corr[k])[0:ny]
             sw[k] = result if base == 0 else jnp.where(left, sw[k], result)
 
-    def corner_of(f, plus, minus, off):
-        low = low_half[0:plus.shape[0]]
-        if f < 4:
-            return rot(jnp.where(low, plus, minus), off - 4 * f, 1)
-        return rot(jnp.where(low, minus, plus), half + off - 4 * (f - 4), 1)
+    def corner_of(f, tile, off):
+        if f < 5:
+            return rot(tile, off - 3 * f, 1)
+        piece = None
+        for at, to, u in spare:
+            piece = pick(piece, slot[0:tile.shape[0]] == at, rot(tile, SEG * (at - to) + off - 3 * u, 1))
+        return piece
 
     with scope("endswait"):
         arrived(12, 5 * ny // 8)
@@ -532,16 +556,21 @@
         with scope("ystrip"):
             if base == 0:
                 y_finish(8, strip_tiles, yd_in)
-            arrived(10 - 9 * base, 4 * (ny // 8 + dx_in.shape[0]))
+            arrived(10 - 9 * base, 2 * ny // 8 + 2 * (ny // 2) // 8 + 4 * dx_in.shape[0])
             off = 8 - 4 * base
+            minus, plus = dr[0, base], dr[1, base]
+            low = low_half[0:ny // 2]
+            own_corner = jnp.concatenate(
+                [jnp.where(low, plus, rot(minus, half, 1)), jnp.where(low, rot(plus, half, 1), minus)], axis=0
+            )
+            cross_corner = jnp.where(low_half[0:8], crossed(dx_in, 1, base), crossed(dx_in, 0, base))
             for f in range(6):
                 t, q = divmod(f, 4)
-                for rows, tile, corners in (
-                    (slice(0, ny), zr[base, t], [dr[i, base] for i in range(2)]),
-                    (halo, crossed(zx_in, base, t), [crossed(dx_in, i, base) for i in range(2)]),
+                for rows, tile, corner in (
+                    (slice(0, ny), zr[base, t], own_corner), (halo, crossed(zx_in, base, t), cross_corner),
                 ):
                     mine = left[0:tile.shape[0]] if base == 0 else ~left[0:tile.shape[0]]
-                    for at, piece in ((2 * base, rot(tile, off - 4 * q, 1)), (2 * base + 1, corner_of(f, corners[1], corners[0], off))):
+                    for at, piece in ((2 * base, rot(tile, off - 4 * q, 1)), (2 * base + 1, corner_of(f, corner, 8 - 3 * base))):
                         st[f, at, rows, :] = jnp.where(mine, st[f, at, rows, :], piece)
 
     late_up = [(upper_in, (i,)) for i in range(4)] + [(e, (4, last + 2))]
@@ -674,9 +703,9 @@
             pltpu.VMEM((4, planes, rows, nz), f32),
             pltpu.VMEM((2, 2, ny, nz), f32),
             pltpu.VMEM((2, 2, ny, nz), f32),
-            pltpu.VMEM((2, 2, ny, nz), f32),
-            pltpu.VMEM((2, 2, ny, nz), f32),
-            pltpu.VMEM((2, 2, 8, nz), f32),
+            pltpu.VMEM((2, 2, ny // 2, nz), f32),
+            pltpu.VMEM((2, 2, ny // 2, nz), f32),
+            pltpu.VMEM((2, 8, nz), f32),
             pltpu.VMEM((sides, 2, 2, 8, nz), f32),
             pltpu.VMEM((2, 2, 8, nz), f32),
             pltpu.VMEM((sides, 2, 2, 8, nz), f32),

time: 12.7 us -> 12.5 us (0.984)
  the two profiles are of different devices: /device:TPU:0 before, /device:TPU:29 now
where the time goes in v10:
time: 12.5 us; the launch traced here: 12.3 us
  Pallas kernels  11.6 us (93%)
  local copies, waits for them, and re-layouts  0.68 us (5%)
    pallas_call x1, Pallas kernels, on_device(): pl.pallas_call(functools.partial(kernel, sizes, nx, ny, nz), out_shape=pl...  11.6 us
    unnamed x1, local copies, waits for them, and re-layouts  0.68 us

profile of v10, /device:TPU:29, one launch (start us, length us, event | category | flops | bytes accessed | tf_op | source)
XLA Modules:
  0.0 12.3 jit_solution(14571153656421445529)
XLA Ops:
  0.0 11.6 %shard_map.55 = f32[3,8,16,128]{3,2,1,0:T(8,128)S(1)} custom-call(f32[8]{0:T(128)} %cond_hbm.1, f32[3,8,16,128]{3,2,1,0:T(8,128)} %rhs_hbm.1, f32[3,8,16,128]{3,2,1,0:T(8,128)} %frac_hbm.1, s32[8,16,128]{2,1,0:T(8,128)} %reg_hbm.1, s32[3,8,16,128]{3,2,1,0:T(8,128)} %flag_hbm.1), custom_call_target="tpu_custom_call" | custom-call | tf_op jit(solution)/shard_map/pallas_call | solution.py:686
  11.6 0.7 %copy.7 = f32[3,8,16,128]{3,2,1,0:T(8,128)} copy(f32[3,8,16,128]{3,2,1,0:T(8,128)S(1)} %shard_map.55) | data formatting | bytes 393216

commit v11 on v10

--- a/solution.py
+++ b/solution.py
@@ -193,6 +193,7 @@
     low_half = lane < half
     quad = (lane % SEG) // 4
     unit = (lane % SEG) // 3
+    fourth = ((0, 6), (3, 7))
     spare = ((0, 3, 0), (1, 3, 3), (2, 3, 4), (nx - 2, 4, 0), (nx - 1, 4, 1))
     left = (lane % SEG) < 8
 
@@ -259,6 +260,9 @@
                 tile = pick(tile, outer & (unit == k), rot(starts[k], 3 * k - off, 1))
             for at, to, u in spare:
                 tile = pick(tile, (slot == to) & (unit == u), rot(packs[5], SEG * (to - at) + 3 * u - off, 1))
+            if side == 0:
+                for f, to in fourth:
+                    tile = pick(tile, (slot == 4) & (lane % SEG == to), rot(packs[f], SEG * (4 - (nx - 1)) + to - 11, 1))
             upper, lower = tile[0:ny // 2], tile[ny // 2:ny]
             ds[0, side] = jnp.where(low_half[0:ny // 2], rot(upper, half, 1), lower)
             ds[1, side] = jnp.where(low_half[0:ny // 2], upper, rot(lower, half, 1))
@@ -523,7 +527,12 @@
 
     def corner_of(f, tile, off):
         if f < 5:
-            return rot(tile, off - 3 * f, 1)
+            piece = rot(tile, off - 3 * f, 1)
+            for k, to in fourth:
+                if off == 8 and k == f:
+                    at = ((slot == nx - 1) & (lane % SEG == 11))[0:tile.shape[0]]
+                    piece = jnp.where(at, rot(tile, SEG * (nx - 1 - 4) + 11 - to, 1), piece)
+            return piece
         piece = None
         for at, to, u in spare:
             piece = pick(piece, slot[0:tile.shape[0]] == at, rot(tile, SEG * (at - to) + off - 3 * u, 1))

time: 12.5 us -> 12.5 us (level)
  no operation moved by 1% of the time
where the time goes in v11:
time: 12.5 us; the launch traced here: 12.3 us
  Pallas kernels  11.6 us (93%)
  local copies, waits for them, and re-layouts  0.68 us (5%)
    pallas_call x1, Pallas kernels, on_device(): pl.pallas_call(functools.partial(kernel, sizes, nx, ny, nz), out_shape=pl...  11.6 us
    unnamed x1, local copies, waits for them, and re-layouts  0.68 us

profile of v11, /device:TPU:29, one launch (start us, length us, event | category | flops | bytes accessed | tf_op | source)
XLA Modules:
  0.0 12.3 jit_solution(17386357079063265119)
XLA Ops:
  0.0 11.6 %shard_map.55 = f32[3,8,16,128]{3,2,1,0:T(8,128)S(1)} custom-call(f32[8]{0:T(128)} %cond_hbm.1, f32[3,8,16,128]{3,2,1,0:T(8,128)} %rhs_hbm.1, f32[3,8,16,128]{3,2,1,0:T(8,128)} %frac_hbm.1, s32[8,16,128]{2,1,0:T(8,128)} %reg_hbm.1, s32[3,8,16,128]{3,2,1,0:T(8,128)} %flag_hbm.1), custom_call_target="tpu_custom_call" | custom-call | tf_op jit(solution)/shard_map/pallas_call | solution.py:695
  11.6 0.7 %copy.7 = f32[3,8,16,128]{3,2,1,0:T(8,128)} copy(f32[3,8,16,128]{3,2,1,0:T(8,128)S(1)} %shard_map.55) | data formatting | bytes 393216

commit v12 on v11

--- a/solution.py
+++ b/solution.py
@@ -338,10 +338,11 @@
         copy(4, e.at[4, first + 1], e.at[4, last + 2], down, False),
         copy(4, e.at[5, first + 1, own_rows], e.at[5, last + 2, own_rows], down, False),
     ]
-    down_first = (lax.rem(pos["gx"], 4) == 1) & (pos["gz"] == 0)
-    wide = (lax.rem(device(gx=-1)["gx"], 4) == 1) & (pos["gz"] == 0)
+    uneven = (pos["gz"] == 0) & (pos["gx"] >= gx % 4 * gx)
+    down_first = (lax.rem(pos["gx"], 4) == 1) & uneven
+    wide = (lax.rem(device(gx=-1)["gx"], 4) == 1) & uneven
     narrow = jnp.logical_not(wide)
-    thin = (lax.rem(device(gx=1)["gx"], 4) == 1) & (pos["gz"] == 0)
+    thin = (lax.rem(device(gx=1)["gx"], 4) == 1) & uneven
 
     def in_order(begin):
         pl.when(down_first)(lambda: begin(0, 1))

time: 12.5 us -> 12.5 us (level)
  no operation moved by 1% of the time
where the time goes in v12:
time: 12.5 us; the launch traced here: 12.3 us
  Pallas kernels  11.6 us (93%)
  local copies, waits for them, and re-layouts  0.68 us (5%)
    pallas_call x1, Pallas kernels, on_device(): pl.pallas_call(functools.partial(kernel, sizes, nx, ny, nz), out_shape=pl...  11.6 us
    unnamed x1, local copies, waits for them, and re-layouts  0.68 us

profile of v12, /device:TPU:29, one launch (start us, length us, event | category | flops | bytes accessed | tf_op | source)
XLA Modules:
  0.0 12.3 jit_solution(4375872792766824823)
XLA Ops:
  0.0 11.6 %shard_map.55 = f32[3,8,16,128]{3,2,1,0:T(8,128)S(1)} custom-call(f32[8]{0:T(128)} %cond_hbm.1, f32[3,8,16,128]{3,2,1,0:T(8,128)} %rhs_hbm.1, f32[3,8,16,128]{3,2,1,0:T(8,128)} %frac_hbm.1, s32[8,16,128]{2,1,0:T(8,128)} %reg_hbm.1, s32[3,8,16,128]{3,2,1,0:T(8,128)} %flag_hbm.1), custom_call_target="tpu_custom_call" | custom-call | tf_op jit(solution)/shard_map/pallas_call | solution.py:696
  11.6 0.7 %copy.7 = f32[3,8,16,128]{3,2,1,0:T(8,128)} copy(f32[3,8,16,128]{3,2,1,0:T(8,128)S(1)} %shard_map.55) | data formatting | bytes 393216

commit v13 on v12

--- a/solution.py
+++ b/solution.py
@@ -244,7 +244,7 @@
                 for f, v in ((k, e[k, first + x, 0:ny, :]), (3 + k, ks)):
                     packs[f] = pick(packs[f], slot == x, end_piece(v, x))
         starts = [jacobi_scale(packs[3 + k]) * packs[k] for k in range(3)]
-        for side, off in ((0, 8), (1, 4)):
+        for side, off in ((1, 4), (0, 8)):
             tiles = [None, None]
             for f in range(6):
                 tiles[f // 4] = pick(tiles[f // 4], quad == f % 4, rot(packs[f], 4 * (f % 4) - off, 1))
@@ -267,11 +267,13 @@
             ds[0, side] = jnp.where(low_half[0:ny // 2], rot(upper, half, 1), lower)
             ds[1, side] = jnp.where(low_half[0:ny // 2], upper, rot(lower, half, 1))
             dx_out[side] = jnp.where(row < 4, tile[0:8], tile[ny - 8:ny])
-        if paired:
-            @pl.when(hurry)
-            def _():
-                pl.when(pos["gy"] == 1)(lambda: pl.semaphore_wait(near.at[1], 1))
-                start_both()
+            if paired:
+                @pl.when(hurry)
+                def _():
+                    if side == 1:
+                        pl.when(pos["gy"] == 1)(lambda: pl.semaphore_wait(near.at[1], 1))
+                    start_far(side)
+                    start(*cross_copies[side])
 
         moves = (
             [(packs[f], 0, 8 * (f // 2) + 3 * (f % 2), 3) for f in range(6)] + [(starts[k], 3, 5 + k, 1) for k in (1, 2)],

time: 12.5 us -> 12.6 us (level)
  no operation moved by 1% of the time
where the time goes in v13:
time: 12.6 us; the launch traced here: 12.4 us
  Pallas kernels  11.7 us (93%)
  local copies, waits for them, and re-layouts  0.68 us (5%)
    pallas_call x1, Pallas kernels, on_device(): pl.pallas_call(functools.partial(kernel, sizes, nx, ny, nz), out_shape=pl...  11.7 us
    unnamed x1, local copies, waits for them, and re-layouts  0.68 us

profile of v13, /device:TPU:29, one launch (start us, length us, event | category | flops | bytes accessed | tf_op | source)
XLA Modules:
  0.0 12.4 jit_solution(13617959032705837555)
XLA Ops:
  0.0 11.7 %shard_map.55 = f32[3,8,16,128]{3,2,1,0:T(8,128)S(1)} custom-call(f32[8]{0:T(128)} %cond_hbm.1, f32[3,8,16,128]{3,2,1,0:T(8,128)} %rhs_hbm.1, f32[3,8,16,128]{3,2,1,0:T(8,128)} %frac_hbm.1, s32[8,16,128]{2,1,0:T(8,128)} %reg_hbm.1, s32[3,8,16,128]{3,2,1,0:T(8,128)} %flag_hbm.1), custom_call_target="tpu_custom_call" | custom-call | tf_op jit(solution)/shard_map/pallas_call | solution.py:698
  11.7 0.7 %copy.7 = f32[3,8,16,128]{3,2,1,0:T(8,128)} copy(f32[3,8,16,128]{3,2,1,0:T(8,128)S(1)} %shard_map.55) | data formatting | bytes 393216

commit v14 on v12

--- a/solution.py
+++ b/solution.py
@@ -311,7 +311,7 @@
     y_start(0, own, ya_out, ya_in)
 
     up, down = device(gx=1), device(gx=-1)
-    ends_copies = [copy(12, ends_out.at[pl.ds(0, 3)], ends_in.at[pl.ds(0, 3)], down, False), copy(12, ends_out.at[pl.ds(3, 2)], ends_in.at[pl.ds(3, 2)], up, False)]
+    ends_copies = [copy(9, ends_out.at[pl.ds(0, 3)], ends_in.at[pl.ds(0, 3)], down, False), copy(9, ends_out.at[pl.ds(3, 2)], ends_in.at[pl.ds(3, 2)], up, False)]
     raw_copies = [
         copy(2, e.at[:, first, own_rows], e.at[:, last + 1, own_rows], down, False),
         copy(3, e.at[:, last, own_rows], e.at[:, first - 1, own_rows], up, False),
@@ -333,7 +333,7 @@
             (e.at[4, first + 1, own_rows], e.at[4, last + 2, own_rows]),
         )
     ]
-    last_copy = copy(9, upper_out.at[pl.ds(4, 2), own_rows], upper_in.at[pl.ds(4, 2), own_rows], down, False)
+    last_copy = copy(4, upper_out.at[pl.ds(4, 2), own_rows], upper_in.at[pl.ds(4, 2), own_rows], down, False)
     mask_copies = [
         copy(4, e.at[4, first + 1], e.at[4, last + 2], down, False),
         copy(4, e.at[5, first + 1, own_rows], e.at[5, last + 2, own_rows], down, False),
@@ -540,7 +540,7 @@
         return piece
 
     with scope("endswait"):
-        arrived(12, 5 * ny // 8)
+        arrived(9, 5 * ny // 8)
     with scope("strippack"):
         for f in range(6):
             t, to = divmod(2 * f, 8)
@@ -592,9 +592,8 @@
 
     def upper_inputs():
         with scope("yup"):
-            pl.when(jnp.logical_not(thin))(lambda: arrived(4, (5 * (ny + 8) + ny) // 8))
+            pl.when(jnp.logical_not(thin))(lambda: arrived(4, (5 * (ny + 8) + 3 * ny) // 8))
             pl.when(thin)(lambda: y_finish(0, late_up, yf_in))
-            arrived(9, 2 * ny // 8)
 
     def lower_side():
         with scope("lower"):
@@ -655,7 +654,7 @@
 
     @pl.when(thin)
     def _():
-        relay("lateup", ((4, 6),), 0, late_up, yf_out, yf_in)
+        relay("lateup", ((4, 8),), 0, late_up, yf_out, yf_in)
 
     def raw_sides():
         with scope("yraw"):
@@ -729,7 +728,7 @@
             pltpu.VMEM((320, 8, nz), f32),
             pltpu.SemaphoreType.DMA((2,)),
             pltpu.SemaphoreType.DMA((1,)),
-            pltpu.SemaphoreType.DMA((13,)),
+            pltpu.SemaphoreType.DMA((12,)),
             pltpu.SemaphoreType.REGULAR((2,)),
         ],
         compiler_params=pltpu.CompilerParams(

time: 12.5 us -> 12.5 us (level)
  no operation moved by 1% of the time
where the time goes in v14:
time: 12.5 us; the launch traced here: 12.3 us
  Pallas kernels  11.6 us (93%)
  local copies, waits for them, and re-layouts  0.68 us (5%)
    pallas_call x1, Pallas kernels, on_device(): pl.pallas_call(functools.partial(kernel, sizes, nx, ny, nz), out_shape=pl...  11.6 us
    unnamed x1, local copies, waits for them, and re-layouts  0.68 us

profile of v14, /device:TPU:29, one launch (start us, length us, event | category | flops | bytes accessed | tf_op | source)
XLA Modules:
  0.0 12.3 jit_solution(10593228754885901486)
XLA Ops:
  0.0 11.6 %shard_map.55 = f32[3,8,16,128]{3,2,1,0:T(8,128)S(1)} custom-call(f32[8]{0:T(128)} %cond_hbm.1, f32[3,8,16,128]{3,2,1,0:T(8,128)} %rhs_hbm.1, f32[3,8,16,128]{3,2,1,0:T(8,128)} %frac_hbm.1, s32[8,16,128]{2,1,0:T(8,128)} %reg_hbm.1, s32[3,8,16,128]{3,2,1,0:T(8,128)} %flag_hbm.1), custom_call_target="tpu_custom_call" | custom-call | tf_op jit(solution)/shard_map/pallas_call | solution.py:695
  11.6 0.7 %copy.7 = f32[3,8,16,128]{3,2,1,0:T(8,128)} copy(f32[3,8,16,128]{3,2,1,0:T(8,128)S(1)} %shard_map.55) | data formatting | bytes 393216
